TPU v7x, 256 devices: a whole 4x4x8 slice. The times are simulated.
256 devices in a mesh: pair: 32 (over z, x), aux: 8 (over y, core).
Axes of the slice: x: 4, y: 4, z: 8, core: 2. Of those that a mesh axis runs over, the one named last changes fastest.
Arguments:
- integrals: bfloat16 [98304, 12288], P('pair', 'aux'), may hold values from -0.15625 to 0.15625
- energy_gaps: float32 [98304], P('pair'), may hold values from 0.3 to 3
- trial_vectors: float32 [98304, 64], P('pair'), may hold values from -160 to 160
Outputs:
- sigma_vectors: float32 [98304, 64], P(('pair', 'aux'))
- subspace: float32 [64, 64], replicated
- residuals: float32 [98304, 64], P(('pair', 'aux'))
- residual_norms: float32 [64], replicated
All inputs are finite; a program needn't handle non-finite values.
Results may differ from a plain program's by a relative error of at most 0.0052.
Values may be sent and summed in bfloat16 or wider, within the bound.
No kernel may reach another device: no remote copies, remote signals or barrier semaphores. Data moves between devices by JAX's collectives and lax.ppermute only.
A program may use at most 64 MiB of HBM per device.

v0:
```python
import jax
import jax.numpy as jnp
from jax import lax
from jax.sharding import Mesh
from jax.sharding import PartitionSpec as P

AUX = ("aux_0", "aux_1")
PAIR = ("pair_0", "pair_1")
PAIR_AUX = ("pair_0", "pair_1", "aux_0", "aux_1")


epsilon = 1e-06


def split_up(value, dim, size):
    lengths = value.shape
    parts = value.reshape(*lengths[:dim], size, lengths[dim] // size, *lengths[dim + 1 :])
    return jnp.moveaxis(parts, dim, 0)


def sent_and_summed(value, axis, dim):
    parts = split_up(value, dim, lax.axis_size(axis))
    arrived = lax.all_to_all(parts, axis, split_axis=0, concat_axis=0, tiled=True)
    return arrived.sum(axis=0)


def copy_for_each(value, axis):
    copies = jnp.broadcast_to(value, (lax.axis_size(axis), *value.shape))
    return lax.all_to_all(copies, axis, split_axis=0, concat_axis=0, tiled=True)


def laid_out(parts, dim):
    parts = jnp.moveaxis(parts, 0, dim)
    lengths = parts.shape
    return parts.reshape(*lengths[:dim], lengths[dim] * lengths[dim + 1], *lengths[dim + 2 :])


def gather_directly(value, axis, dim):
    parts = copy_for_each(value, axis)
    return laid_out(parts, dim)


def summed_on_arrival(value, axis, dim):
    size = lax.axis_size(axis)
    parts = lax.all_to_all(split_up(value, dim, size), axis, 0, 0, tiled=True)
    return jnp.sum(parts.astype(jnp.float32), axis=0)


def taken_together(value, axis):
    return copy_for_each(value, axis).sum(axis=0)


def one_axis_at_a_time(value, axes):
    far, near = axes
    nearer = taken_together(value, near)
    return taken_together(nearer, far)


def packed_total(arrays, axis):
    ends = [0]
    for a in arrays:
        ends.append(ends[-1] + a.size)
    running = one_axis_at_a_time(jnp.concatenate([a.ravel() for a in arrays]), axis)
    return tuple((running[b:e].reshape(a.shape) for a, b, e in zip(arrays, ends, ends[1:])))


def local(integrals, energy_gaps, trial_vectors):
    pair_rows = trial_vectors.shape[0]
    row_share = pair_rows // lax.axis_size(AUX)
    total_pairs = float(pair_rows * lax.axis_size(PAIR))
    trial_half = trial_vectors.astype(jnp.bfloat16)
    partial_value = lax.dot_general(
        integrals, trial_half, (((0,), (0,)), ((), ())), preferred_element_type=jnp.float32
    )
    shares = sent_and_summed(partial_value, PAIR, 0).astype(jnp.bfloat16)
    terms = jnp.dot(integrals, gather_directly(shares, PAIR, 0), preferred_element_type=jnp.float32)
    coupled = summed_on_arrival(terms.astype(jnp.bfloat16), AUX, 0)
    first_own = lax.axis_index(AUX) * row_share
    own_trial = lax.dynamic_slice_in_dim(trial_vectors, first_own, row_share, 0)
    own_gaps = lax.dynamic_slice_in_dim(energy_gaps, first_own, row_share, 0)
    sigma_rows = own_gaps[:, None] * own_trial + 2.0 * coupled
    products = lax.dot_general(
        own_trial,
        sigma_rows,
        (((0,), (0,)), ((), ())),
        precision=lax.Precision.HIGHEST,
        preferred_element_type=jnp.float32,
    )
    squares = jnp.sum(own_trial * own_trial, axis=0)
    sigma_sq = jnp.sum(sigma_rows * sigma_rows, axis=0)
    products, squares, sigma_sq = packed_total(
        (products, squares, sigma_sq), (("pair_0", "pair_1"), ("aux_0", "aux_1"))
    )
    subspace = products / total_pairs
    rayleigh = jnp.diagonal(subspace) / (squares / total_pairs + epsilon)
    residual_rows = sigma_rows - own_trial * rayleigh[None, :]
    residual_sq = sigma_sq - 2.0 * rayleigh * jnp.diagonal(products) + rayleigh * rayleigh * squares
    residual_norms = jnp.sqrt(residual_sq / total_pairs + epsilon)
    return (sigma_rows, subspace, residual_rows, residual_norms)


def solution(mesh):
    finer = Mesh(mesh.devices.reshape(8, 4, 4, 2), ("pair_0", "pair_1", "aux_0", "aux_1"))
    return jax.shard_map(
        local,
        mesh=finer,
        in_specs=(P(PAIR, AUX), P(PAIR), P(PAIR, None)),
        out_specs=(P(PAIR_AUX, None), P(), P(PAIR_AUX, None), P()),
        check_vma=False,
    )
```

profile of v0, /device:TPU:2, one launch (start us, length us, event | category | flops | bytes accessed | tf_op | source)
XLA Modules:
  0.0 111.1 jit_solution(3957253671500624351)
XLA Ops:
  0.6 6.5 %fusion = f32[1536,64]{1,0:T(8,128)S(1)} fusion(bf16[3072,1536]{1,0:T(8,128)(2,1)} %param.3, f32[3072,64]{0,1:T(8,128)} %param.5), kind=kOutput, calls=%fused_computation.5 | convolution fusion | flops 604176384 | bytes 10616832 | tf_op jit(solution)/shard_map/reshape | solution.py:17
  7.1 0.5 reshape.58
  7.6 25.4 %all_to_all.27 = f32[32,1,3072]{2,1,0:T(1,128)S(1)} all-to-all(f32[32,1,3072]{2,1,0:T(1,128)S(1)} %reshape.58), channel_id=1, replica_groups=mesh['pair_0'=8,'pair_1'=4,'aux_0'=4,'aux_1'=2] {'pair_0','pair_1'}, dimensions={0} | all-to-all | bytes 786432 | tf_op jit(solution)/shard_map/all_to_all | solution.py:23
  33.0 0.5 broadcast.62
  33.6 1.6 %reduce.2 = f32[32,3072]{1,0:T(8,128)S(1)} reduce(f32[32,1,3072]{2,1,0:T(1,128)S(1)} %all_to_all.27, f32[]{:T(128)} %broadcast.62), dimensions={1}, to_apply=%all_to_all.17.reduce_sub_computation | reduce | bytes 786436 | tf_op jit(solution)/shard_map/all_to_all | solution.py:23
  35.1 0.2 reshape.59
  35.3 0.1 reduce_sum.54
  35.4 0.1 broadcast_in_dim.17
  35.5 0.2 reshape.60
  35.7 14.7 %all_to_all.28 = bf16[32,2,1536]{2,1,0:T(2,128)(2,1)S(1)} all-to-all(bf16[32,2,1536]{2,1,0:T(2,128)(2,1)S(1)} %reshape.60), channel_id=1, replica_groups=mesh['pair_0'=8,'pair_1'=4,'aux_0'=4,'aux_1'=2] {'pair_0','pair_1'}, dimensions={0} | all-to-all | bytes 393216 | tf_op jit(solution)/shard_map/all_to_all | solution.py:29
  50.4 0.3 reshape.61
  50.7 6.7 %convolution_convert_fusion = bf16[64,3072]{1,0:T(8,128)(2,1)S(1)} fusion(bf16[1536,64]{1,0:T(8,128)(2,1)S(1)} %bitcast.14, bf16[3072,1536]{1,0:T(8,128)(2,1)} %param.3), kind=kOutput, calls=%fused_computation.2 | convolution fusion | flops 604176384 | bytes 10027008 | tf_op jit(solution)/shard_map/dot_general | solution.py:76
  57.3 0.8 copy.36
  58.1 4.5 %all-to-all-start.2 = ((bf16[8,384,64]{1,2,0:T(8,128)(2,1)}), bf16[8,384,64]{1,2,0:T(8,128)(2,1)S(1)}, u32[]{:S(2)}, u32[]{:S(2)}) async-start(bf16[8,384,64]{1,2,0:T(8,128)(2,1)} %bitcast.12), calls=%async_computation.2 | async-start | bytes 786432 | tf_op jit(solution)/shard_map/all_to_all | solution.py:45
  62.6 0.8 dynamic_slice.6
  63.4 8.1 %all-to-all-done.2 = bf16[8,384,64]{1,2,0:T(8,128)(2,1)S(1)} async-done(((bf16[8,384,64]{1,2,0:T(8,128)(2,1)}), bf16[8,384,64]{1,2,0:T(8,128)(2,1)S(1)}, u32[]{:S(2)}, u32[]{:S(2)}) %all-to-all-start.2) | async-done | bytes 393248 | tf_op jit(solution)/shard_map/all_to_all | solution.py:45
  71.6 1.0 multiply_reduce_fusion
  72.6 1.2 %fusion.2 = f32[64,64]{1,0:T(8,128)S(1)} fusion(f32[384,64]{0,1:T(8,128)S(1)} %get-tuple-element.7, f32[3072,64]{0,1:T(8,128)} %param.5, s32[]{:T(128)S(6)} %select_n.10), kind=kOutput, calls=%fused_computation.11 | convolution fusion | flops 18874368 | bytes 212996 | tf_op jit(solution)/shard_map/dot_general | solution.py:82
  73.8 0.1 reshape.44
  73.8 0.1 concatenate.8
  73.9 0.1 broadcast_in_dim.18
  74.0 8.5 %all_to_all.29 = f32[8,1,4224]{2,1,0:T(1,128)S(1)} all-to-all(f32[8,1,4224]{2,1,0:T(1,128)S(1)} %broadcast_in_dim.18), channel_id=1, replica_groups=mesh['pair_0'=8,'pair_1'=4,'aux_0'=4,'aux_1'=2] {'aux_0','aux_1'}, dimensions={0} | all-to-all | bytes 270336 | tf_op jit(solution)/shard_map/all_to_all | solution.py:29
  82.5 0.1 reduce_sum.58
  82.6 1.1 broadcast_in_dim.19
  83.7 5.8 %all-to-all-start.4 = ((f32[32,1,4224]{2,1,0:T(1,128)}), f32[32,1,4224]{2,1,0:T(1,128)S(1)}, u32[]{:S(2)}, u32[]{:S(2)}) async-start(f32[32,1,4224]{2,1,0:T(1,128)} %broadcast_in_dim.19), calls=%async_computation.4 | async-start | bytes 1081344 | tf_op jit(solution)/shard_map/all_to_all | solution.py:29
  89.5 17.3 %all-to-all-done.4 = f32[32,1,4224]{2,1,0:T(1,128)S(1)} async-done(((f32[32,1,4224]{2,1,0:T(1,128)}), f32[32,1,4224]{2,1,0:T(1,128)S(1)}, u32[]{:S(2)}, u32[]{:S(2)}) %all-to-all-start.4) | async-done | bytes 540704 | tf_op jit(solution)/shard_map/all_to_all | solution.py:29
  106.8 0.3 reduce_sum.59
  107.2 0.1 reshape.45
  107.2 0.8 gather_fusion.1
  108.1 0.8 gather_fusion
  108.9 0.6 add_sqrt_fusion
  109.5 1.6 %multiply_subtract_fusion = f32[384,64]{0,1:T(8,128)} fusion(f32[384,64]{0,1:T(8,128)S(1)} %get-tuple-element.7, f32[3072,64]{0,1:T(8,128)} %param.5, s32[]{:T(128)S(6)} %select_n.10, f32[64]{0:T(128)S(1)} %get-tuple-element.5), kind=kLoop, calls=%fused_computation.7 | loop fusion | flops 49152 | bytes 295172 | tf_op jit(solution)/shard_map/sub | solution.py:96
  (8 shorter events, 0.1 us)
Async XLA Ops:
  58.1 13.4 %all-to-all-start.2 = ((bf16[8,384,64]{1,2,0:T(8,128)(2,1)}), bf16[8,384,64]{1,2,0:T(8,128)(2,1)S(1)}, u32[]{:S(2)}, u32[]{:S(2)}) async-start(bf16[8,384,64]{1,2,0:T(8,128)(2,1)} %bitcast.12), calls=%async_computation.2 | async-start | bytes 786432 | tf_op jit(solution)/shard_map/all_to_all | solution.py:45
  72.6 38.5 %copy-start.1 = (f32[384,64]{0,1:T(8,128)}, f32[384,64]{0,1:T(8,128)S(1)}, u32[]{:S(2)}) copy-start(f32[384,64]{0,1:T(8,128)S(1)} %get-tuple-element.7) | copy-start | bytes 294916
  83.7 23.1 %all-to-all-start.4 = ((f32[32,1,4224]{2,1,0:T(1,128)}), f32[32,1,4224]{2,1,0:T(1,128)S(1)}, u32[]{:S(2)}, u32[]{:S(2)}) async-start(f32[32,1,4224]{2,1,0:T(1,128)} %broadcast_in_dim.19), calls=%async_computation.4 | async-start | bytes 1081344 | tf_op jit(solution)/shard_map/all_to_all | solution.py:29
  107.2 3.8 %copy-start = (f32[64,64]{1,0:T(8,128)}, f32[64,64]{1,0:T(8,128)S(1)}, u32[]{:S(2)}) copy-start(f32[64,64]{1,0:T(8,128)S(1)} %broadcast_multiply_fusion) | copy-start | bytes 49156
where the time goes:
time: 112 us; the launch traced here: 111 us
  blocking collectives  48.6 us (43%)
  waiting for transfers between devices  25.5 us (23%)
  matrix products  14.3 us (13%)
  starting transfers between devices  10.2 us (9%)
  local copies, waits for them, and re-layouts  6.32 us (6%)
  other arithmetic  5.36 us (5%)
    all_to_all x1, blocking collectives, sent_and_summed(): lax.all_to_all(parts, axis, split_axis=0, concat_axis=0, tiled=True)  25.4 us
    all_to_all x2, blocking collectives, copy_for_each(): return lax.all_to_all(copies, axis, split_axis=0, concat_axis=0, tiled=True)  23.2 us
    all_to_all x1, waiting for transfers between devices, copy_for_each(): return lax.all_to_all(copies, axis, split_axis=0, concat_axis=0, tiled=True)  17.3 us
    all_to_all x1, waiting for transfers between devices, summed_on_arrival(): parts = lax.all_to_all(split_up(value, dim, size), axis, 0, 0, tiled=True)  8.14 us
    dot_general x1, matrix products, local(): jnp.dot(integrals, gather_directly(shares, PAIR, 0), preferred_element_ty...  6.65 us
    reshape x1, matrix products, split_up(): value.reshape(*lengths[:dim], size, lengths[dim] // size, *lengths[dim +...  6.48 us
    all_to_all x1, starting transfers between devices, copy_for_each(): return lax.all_to_all(copies, axis, split_axis=0, concat_axis=0, tiled=True)  5.77 us
    all_to_all x1, starting transfers between devices, summed_on_arrival(): parts = lax.all_to_all(split_up(value, dim, size), axis, 0, 0, tiled=True)  4.47 us
  transfers between devices with their start and end apart: 2, of which 2 were waited for; matrix products, arithmetic and copies ran while one was open for 1% of the time, Pallas kernels for 0%

commit v1 on v0

v1 whole, which is shorter than its diff:
```python
import jax
import jax.numpy as jnp
from jax import lax
from jax.experimental import pallas as pl
from jax.experimental.pallas import tpu as pltpu
from jax.sharding import Mesh
from jax.sharding import PartitionSpec as P

PAIR = ("z", "x")
AUX = ("y", "c")
ALL = ("z", "x", "y", "c")

epsilon = 1e-06
BF = jnp.bfloat16
F32 = jnp.float32
NT = (((1,), (1,)), ((), ()))
VMEM = pl.BlockSpec(memory_space=pltpu.VMEM)
HBM = pl.BlockSpec(memory_space=pltpu.HBM)
CHUNKS = 12
FLIGHT = 6
TOTALS_LIMIT = 60 * 1024 * 1024
COUPLED_LIMIT = 46 << 20


def split_two(value):
    high = value.astype(BF).astype(F32)
    return high, (value - high).astype(BF).astype(F32)


def totals_kernel(groups, integrals, trial, gaps, out, held, x_ref, gap_ref, stats, sems, small):
    pairs, aux = integrals.shape
    rows = pairs // CHUNKS

    def copy(n):
        return pltpu.make_async_copy(integrals.at[pl.ds(n * rows, rows)], held.at[pl.ds(n * rows, rows)], sems.at[n])

    x_copy = pltpu.make_async_copy(trial, x_ref, small.at[0])
    gap_copy = pltpu.make_async_copy(gaps, gap_ref, small.at[1])
    x_copy.start()
    gap_copy.start()
    for n in range(FLIGHT):
        copy(n).start()
    x_copy.wait()
    gap_copy.wait()
    x = x_ref[...]
    gx = x * gap_ref[...]
    x_high, x_low = split_two(x)
    g_high, g_low = split_two(gx)
    half = x_high.astype(BF)
    low = x_low.astype(BF)
    left = jnp.concatenate([half, low], axis=0)
    right = jnp.concatenate([g_high.astype(BF), g_low.astype(BF)], axis=0)
    both = lax.dot_general(left, right, NT, preferred_element_type=F32)
    vecs = x.shape[0]
    gram = both[:vecs, :vecs] + both[:vecs, vecs:] + both[vecs:, :vecs]
    squares = jnp.sum(x * x, axis=1, keepdims=True)
    wide = jnp.concatenate([gram, jnp.broadcast_to(squares, (vecs, vecs))], axis=1)
    high, low_part = split_two(wide)
    per = vecs // groups
    stats[...] = jnp.zeros_like(stats)
    for j in range(groups):
        stats[j, 0:per, :] = high[j * per : (j + 1) * per]
        stats[j, per : 2 * per, :] = low_part[j * per : (j + 1) * per]
    total = None
    for n in range(CHUNKS):
        copy(n).wait()
        if n + FLIGHT < CHUNKS:
            copy(n + FLIGHT).start()
        block = held[n * rows : (n + 1) * rows, :]
        part = jnp.dot(half[:, n * rows : (n + 1) * rows], block, preferred_element_type=F32)
        total = part if total is None else total + part
    columns = aux // 128
    tiles = (vecs // 8) * columns
    each = tiles // groups
    for t in range(tiles):
        r, q = divmod(t, columns)
        j, i = divmod(t, each)
        out[j, 8 * i : 8 * i + 8, :] = total[8 * r : 8 * r + 8, 128 * q : 128 * q + 128].astype(BF)
    out[:, 8 * each : 8 * each + 8, :] = stats[...].astype(BF)


def totals(integrals, trial, gaps, groups):
    pairs, aux = integrals.shape
    vecs = trial.shape[0]
    tall = (vecs // 8) * (aux // 128) // groups * 8 + 8
    return pl.pallas_call(
        lambda *refs: totals_kernel(groups, *refs),
        out_shape=jax.ShapeDtypeStruct((groups, tall, 128), BF),
        in_specs=[HBM, HBM, HBM],
        out_specs=VMEM,
        scratch_shapes=[
            pltpu.VMEM((pairs, aux), BF),
            pltpu.VMEM((vecs, pairs), F32),
            pltpu.VMEM((1, pairs), F32),
            pltpu.VMEM((groups, 8, 128), F32),
            pltpu.SemaphoreType.DMA((CHUNKS,)),
            pltpu.SemaphoreType.DMA((2,)),
        ],
        compiler_params=pltpu.CompilerParams(vmem_limit_bytes=TOTALS_LIMIT),
        cost_estimate=pl.CostEstimate(flops=2 * pairs * aux * 256, bytes_accessed=2 * pairs * aux, transcendentals=0),
        name="totals",
    )(integrals, trial, gaps)


def share(parts, per):
    total = jnp.sum(parts.astype(F32), axis=0)
    base = total.shape[0] - 8
    stat = total[base : base + per] + total[base + per : base + 2 * per]
    high = lax.reduce_precision(stat, 8, 7)
    tail = jnp.concatenate([high, stat - high, jnp.zeros((8 - 2 * per, 128), F32)], axis=0)
    mine = jnp.concatenate([total[:base], tail], axis=0).astype(BF)
    return jnp.broadcast_to(mine[None], parts.shape)


def aux_rows(gathered, rows):
    vecs, aux = rows.shape
    groups = gathered.shape[0]
    columns = aux // 128
    tiles = (vecs // 8) * columns
    each = tiles // groups
    for t in range(tiles):
        r, q = divmod(t, columns)
        j, i = divmod(t, each)
        rows[8 * r : 8 * r + 8, 128 * q : 128 * q + 128] = gathered[j, 8 * i : 8 * i + 8, :]


def coupled_kernel(integrals, kept, gathered, other, own, rows, held, sems):
    ys, cs = lax.axis_size("y"), lax.axis_size("c")
    block_rows = integrals.shape[0] // ys
    share_rows = block_rows // cs
    y, c = lax.axis_index("y"), lax.axis_index("c")
    copies = []
    for n in range(1, ys):
        copies.append(pltpu.make_async_copy(integrals.at[pl.ds(n * block_rows, block_rows)], held.at[n - 1], sems.at[n - 1]))
        copies[-1].start()
    aux_rows(gathered, rows)
    a = rows[...]
    gram = lax.dot_general(a, a, NT, preferred_element_type=F32)
    high, low = split_two(jnp.concatenate([gram, gram], axis=1))
    none = jnp.zeros((a.shape[0], share_rows), F32)
    own[ys] = jnp.concatenate([none, low], axis=1)
    other[ys] = jnp.concatenate([none, low], axis=1).astype(BF)
    for n in range(ys):
        if n:
            copies[n - 1].wait()
        source = held[n - 1] if n else kept[...]
        block = lax.dot_general(a, source, NT, preferred_element_type=F32)
        left, right = block[:, :share_rows], block[:, share_rows:]
        to = lax.rem(n + ys - y, ys)
        own[to] = jnp.concatenate([jnp.where(c == 0, left, right), high], axis=1)
        other[to] = jnp.concatenate([jnp.where(c == 0, right, left), high], axis=1).astype(BF)


def coupled(integrals, kept, gathered, vecs):
    pairs, aux = integrals.shape
    ys = lax.axis_size("y")
    block_rows = pairs // ys
    wide = block_rows // lax.axis_size("c") + 2 * vecs
    return pl.pallas_call(
        coupled_kernel,
        out_shape=[
            jax.ShapeDtypeStruct((ys + 1, vecs, wide), BF),
            jax.ShapeDtypeStruct((ys + 1, vecs, wide), F32),
        ],
        in_specs=[HBM, VMEM, VMEM],
        out_specs=[VMEM, VMEM],
        scratch_shapes=[
            pltpu.VMEM((vecs, aux), BF),
            pltpu.VMEM((ys - 1, block_rows, aux), BF),
            pltpu.SemaphoreType.DMA((ys - 1,)),
        ],
        compiler_params=pltpu.CompilerParams(vmem_limit_bytes=COUPLED_LIMIT),
        cost_estimate=pl.CostEstimate(flops=2 * pairs * aux * 256, bytes_accessed=2 * pairs * aux, transcendentals=0),
        name="coupled",
    )(integrals, kept, gathered)


def deal(own, other, vecs):
    ys, wide = own.shape[0] - 1, own.shape[2]
    total = own + other.astype(F32)
    total = total[:ys] + total[ys:]
    lane = lax.broadcasted_iota(jnp.int32, total.shape, 2)
    high = lax.reduce_precision(total, 8, 7)
    low = lax.reduce_precision(total - high, 8, 7)
    parts = jnp.where(lane < wide - vecs, high, low)
    mine = jnp.where(lane[0] < wide - 2 * vecs, total[0], parts[0])
    return mine, *[parts[k].astype(BF) for k in range(1, ys)]


def sigma_kernel(total_pairs, per, gathered, trial, gaps, kept, one, two, three, sigma, subspace, residuals, norms, grams):
    ys = 4
    y = lax.axis_index("y")
    vecs, rows = trial.shape
    block = kept[:, :rows]
    for part in (one, two, three):
        block = block + part[:, :rows].astype(F32)
    for k, part in enumerate((kept, one, two, three)):
        grams[lax.rem(y + ys - k, ys)] = part[:, rows:].astype(F32)
    gram = grams[0] + grams[1] + grams[2] + grams[3]
    gram = gram[:, :vecs] + gram[:, vecs:]
    groups, tall, _ = gathered.shape
    base = tall - 8
    wide = jnp.concatenate(
        [gathered[j, base : base + per, :].astype(F32) + gathered[j, base + per : base + 2 * per, :].astype(F32) for j in range(groups)],
        axis=0,
    )
    products = (wide[:, :vecs] + 2.0 * gram) / total_pairs
    subspace[...] = products
    r = lax.broadcasted_iota(jnp.int32, (vecs, vecs), 0)
    q = lax.broadcasted_iota(jnp.int32, (vecs, vecs), 1)
    diagonal = jnp.sum(jnp.where(r == q, products, 0.0), axis=1, keepdims=True)
    rayleigh = diagonal / (wide[:, vecs : vecs + 1] / total_pairs + epsilon)
    x = trial[...]
    s = gaps[...] * x + 2.0 * block
    sigma[...] = s
    rest = s - rayleigh * x
    residuals[...] = rest
    sums = jnp.sum(rest * rest, axis=1, keepdims=True)
    line = jnp.sum(jnp.where(r == q, jnp.broadcast_to(sums, (vecs, vecs)), 0.0), axis=0, keepdims=True)
    norms[...] = jnp.concatenate([line, jnp.zeros_like(line)], axis=1)


def sigma_rows(total_pairs, per, gathered, trial, gaps, parts):
    vecs, rows = trial.shape
    return pl.pallas_call(
        lambda *refs: sigma_kernel(total_pairs, per, *refs),
        out_shape=[
            jax.ShapeDtypeStruct((vecs, rows), F32),
            jax.ShapeDtypeStruct((vecs, vecs), F32),
            jax.ShapeDtypeStruct((vecs, rows), F32),
            jax.ShapeDtypeStruct((1, 128), F32),
        ],
        in_specs=[VMEM] * 7,
        out_specs=[VMEM] * 4,
        scratch_shapes=[pltpu.VMEM((4, vecs, 128), F32)],
        compiler_params=pltpu.CompilerParams(vmem_limit_bytes=16 << 20),
        cost_estimate=pl.CostEstimate(flops=20 * trial.size, bytes_accessed=16 * trial.size, transcendentals=0),
        name="sigma_rows",
    )(gathered, trial, gaps, *parts)


def exchange(value, axis):
    return lax.all_to_all(value, axis, 0, 0, tiled=True)


def shifted(value, axis, by):
    n = lax.axis_size(axis)
    return lax.ppermute(value, axis, [(i, (i + by) % n) for i in range(n)])


def local(integrals, energy_gaps, trial_vectors):
    pairs, vecs = trial_vectors.shape
    groups = lax.axis_size(PAIR)
    ys, cs = lax.axis_size("y"), lax.axis_size("c")
    total_pairs = float(pairs * groups)
    per = vecs // groups
    share_rows = pairs // (ys * cs)
    trial = trial_vectors.T
    gaps = energy_gaps.reshape(1, pairs)
    parts = totals(integrals, trial, gaps, groups)
    mine = share(exchange(parts, PAIR), per)
    gathered = exchange(mine, PAIR)
    other, own = coupled(integrals, lax.slice_in_dim(integrals, 0, pairs // ys, axis=0), gathered, vecs)
    arrived = shifted(other, "c", 1)
    mine, *sent = deal(own, arrived, vecs)
    came = [shifted(block, "y", k + 1) for k, block in enumerate(sent)]
    first = (lax.axis_index("y") * cs + lax.axis_index("c")) * share_rows
    own_trial = lax.dynamic_slice_in_dim(trial, first, share_rows, 1)
    own_gaps = lax.dynamic_slice_in_dim(gaps, first, share_rows, 1)
    sigma, subspace, residuals, norms = sigma_rows(total_pairs, per, gathered, own_trial, own_gaps, [mine, *came])
    norms = norms + shifted(norms, "c", 1)
    everyone = ("z", "x", "y")
    copies = jnp.broadcast_to(norms, (lax.axis_size(everyone), 1, 128))
    sums = jnp.sum(exchange(copies, everyone), axis=(0, 1))[:vecs]
    residual_norms = jnp.sqrt(sums / total_pairs + epsilon)
    return (sigma.T, subspace, residuals.T, residual_norms)


def solution(mesh):
    finer = Mesh(mesh.devices.reshape(8, 4, 4, 2), ALL)
    return jax.shard_map(
        local,
        mesh=finer,
        in_specs=(P(PAIR, AUX), P(PAIR), P(PAIR, None)),
        out_specs=(P(ALL, None), P(), P(ALL, None), P()),
        check_vma=False,
    )
```

time: 112 us -> 86.8 us (0.78)
  blocking collectives: 48.6 us -> 19.9 us
  matrix products: 14.3 us -> 0 us
  starting transfers between devices: 10.2 us -> 23.2 us
  Pallas kernels: 0 us -> 12.8 us
  other arithmetic: 5.36 us -> 0.98 us
  local copies, waits for them, and re-layouts: 6.32 us -> 4.39 us
  waiting for transfers between devices: 25.5 us -> 23.7 us
    all_to_all x3 -> x1, blocking collectives: 48.6 us -> 19.9 us  [exchange(): return lax.all_to_all(value, axis, 0, 0, tiled=True)]
    pallas_call x0 -> x3, Pallas kernels: none -> 12.8 us  [the longest x1 6.72 us: totals(): pl.pallas_call(lambda *refs: totals_kernel(groups, *refs), out_shape=jax....]
    dot_general x2 -> x0, matrix products: 7.83 us -> none  [the longest x1 6.65 us: local(): jnp.dot(integrals, gather_directly(shares, PAIR, 0), preferred_element_ty...]
    all_to_all x2, starting transfers between devices: 10.2 us -> 17.2 us  [exchange(): return lax.all_to_all(value, axis, 0, 0, tiled=True)]
    all_to_all x2, waiting for transfers between devices: 25.5 us -> 19 us  [exchange(): return lax.all_to_all(value, axis, 0, 0, tiled=True)]
    reshape x1 -> x0, matrix products: 6.48 us -> none  [split_up(): value.reshape(*lengths[:dim], size, lengths[dim] // size, *lengths[dim +...]
    ppermute x0 -> x5, starting transfers between devices: none -> 6 us  [shifted(): return lax.ppermute(value, axis, [(i, (i + by) % n) for i in range(n)])]
    ppermute x0 -> x5, waiting for transfers between devices: none -> 4.73 us  [shifted(): return lax.ppermute(value, axis, [(i, (i + by) % n) for i in range(n)])]
  transfers between devices with their start and end apart: 2 -> 7, of which waited for: 2 -> 6; matrix products, arithmetic and copies ran while one was open for 1% -> 4% of each run, Pallas kernels for 0% -> 0%
where the time goes in v1:
time: 86.8 us; the launch traced here: 85.8 us
  waiting for transfers between devices  23.7 us (27%)
  starting transfers between devices  23.2 us (27%)
  blocking collectives  19.9 us (23%)
  Pallas kernels  12.8 us (15%)
  local copies, waits for them, and re-layouts  4.39 us (5%)
  other arithmetic  0.98 us (1%)
    all_to_all x1, blocking collectives, exchange(): return lax.all_to_all(value, axis, 0, 0, tiled=True)  19.9 us
    all_to_all x2, waiting for transfers between devices, exchange(): return lax.all_to_all(value, axis, 0, 0, tiled=True)  19 us
    all_to_all x2, starting transfers between devices, exchange(): return lax.all_to_all(value, axis, 0, 0, tiled=True)  17.2 us
    pallas_call x1, Pallas kernels, totals(): pl.pallas_call(lambda *refs: totals_kernel(groups, *refs), out_shape=jax....  6.72 us
    ppermute x5, starting transfers between devices, shifted(): return lax.ppermute(value, axis, [(i, (i + by) % n) for i in range(n)])  6 us
    pallas_call x1, Pallas kernels, coupled(): pl.pallas_call(coupled_kernel, out_shape=[jax.ShapeDtypeStruct((ys + 1, v...  5.19 us
    ppermute x5, waiting for transfers between devices, shifted(): return lax.ppermute(value, axis, [(i, (i + by) % n) for i in range(n)])  4.73 us
    slice x1, local copies, waits for them, and re-layouts, local(): lax.slice_in_dim(integrals, 0, pairs // ys, axis=0)  1.82 us
  transfers between devices with their start and end apart: 7, of which 6 were waited for; matrix products, arithmetic and copies ran while one was open for 4% of the time, Pallas kernels for 0%

profile of v1, /device:TPU:2, one launch (start us, length us, event | category | flops | bytes accessed | tf_op | source)
XLA Modules:
  0.0 85.8 jit_solution(1118869679509680669)
XLA Ops:
  0.6 6.7 %totals.1 = bf16[32,32,128]{2,1,0:T(8,128)(2,1)} custom-call(bf16[3072,1536]{1,0:T(8,128)(2,1)} %integrals.1, f32[64,3072]{1,0:T(8,128)} %bitcast.25, f32[1,3072]{1,0:T(1,128)} %bitcast.27), custom_call_target="tpu_custom_call" | custom-call | flops 2415919104 | bytes 9437184 | tf_op jit(solution)/shard_map/totals/pallas_call | solution.py:86
  7.4 11.6 %all-to-all-start = ((bf16[32,32,128]{2,1,0:T(8,128)(2,1)}), bf16[32,32,128]{2,1,0:T(8,128)(2,1)S(1)}, u32[]{:S(2)}, u32[]{:S(2)}) async-start(bf16[32,32,128]{2,1,0:T(8,128)(2,1)} %totals.1), calls=%async_computation | async-start | bytes 524288 | tf_op jit(solution)/shard_map/all_to_all | solution.py:243
  19.0 0.1 pad.3.clone
  19.1 11.1 %all-to-all-done = bf16[32,32,128]{2,1,0:T(8,128)(2,1)S(1)} async-done(((bf16[32,32,128]{2,1,0:T(8,128)(2,1)}), bf16[32,32,128]{2,1,0:T(8,128)(2,1)S(1)}, u32[]{:S(2)}, u32[]{:S(2)}) %all-to-all-start) | async-done | bytes 262176 | tf_op jit(solution)/shard_map/all_to_all | solution.py:243
  30.3 0.1 maximum_maximum_fusion
  30.4 0.7 broadcast_in_dim.13
  31.1 5.6 %all-to-all-start.1 = ((bf16[32,32,128]{2,1,0:T(8,128)(2,1)}), bf16[32,32,128]{2,1,0:T(8,128)(2,1)S(1)}, u32[]{:S(2)}, u32[]{:S(2)}) async-start(bf16[32,32,128]{2,1,0:T(8,128)(2,1)} %broadcast_in_dim.13), calls=%async_computation.1 | async-start | bytes 524288 | tf_op jit(solution)/shard_map/all_to_all | solution.py:243
  36.7 1.8 %slice.44.kept = bf16[768,1536]{1,0:T(8,128)(2,1)S(1)} slice(bf16[3072,1536]{1,0:T(8,128)(2,1)} %integrals.1), slice={[0:768], [0:1536]} | slice | bytes 4718592 | tf_op jit(solution)/shard_map/slice | solution.py:263
  38.5 0.8 dynamic-slice.7
  39.3 7.8 %all-to-all-done.1.gathered.refs_0_ = bf16[32,32,128]{2,1,0:T(8,128)(2,1)S(1)} async-done(((bf16[32,32,128]{2,1,0:T(8,128)(2,1)}), bf16[32,32,128]{2,1,0:T(8,128)(2,1)S(1)}, u32[]{:S(2)}, u32[]{:S(2)}) %all-to-all-start.1) | async-done | bytes 262176 | tf_op jit(solution)/shard_map/all_to_all | solution.py:243
  47.1 5.2 %coupled.1 = (bf16[5,64,512]{2,1,0:T(8,128)(2,1)S(1)}, f32[5,64,512]{2,1,0:T(8,128)S(1)}) custom-call(bf16[3072,1536]{1,0:T(8,128)(2,1)} %integrals.1, bf16[768,1536]{1,0:T(8,128)(2,1)S(1)} %slice.44.kept, bf16[32,32,128]{2,1,0:T(8,128)(2,1)S(1)} %all-to-all-done.1.gathered.refs_0_), custom_call_target="tpu_custom_call" | custom-call | flops 2415919104 | bytes 9437184 | tf_op jit(solution)/shard_map/coupled/pallas_call | solution.py:159
  52.3 0.1 collective-permute-start
  52.4 0.9 %dynamic-slice_bitcast_fusion.refs_1_ = f32[64,384]{1,0:T(8,128)S(1)} fusion(f32[3072,64]{0,1:T(8,128)} %param.5, s32[]{:T(128)S(6)} %select_n.12), kind=kLoop, calls=%fused_computation.10 | loop fusion | bytes 196612 | tf_op jit(solution)/shard_map/dynamic_slice | solution.py:268
  53.3 0.7 collective-permute-done
  54.0 0.1 convert_add_fusion
  54.1 0.2 fusion.3
  54.3 1.7 %collective-permute-start.1 = (bf16[64,512]{1,0:T(8,128)(2,1)S(1)}, bf16[64,512]{1,0:T(8,128)(2,1)S(1)}, u32[]{:S(2)}, u32[]{:S(2)}) collective-permute-start(bf16[64,512]{1,0:T(8,128)(2,1)S(1)} %get-tuple-element.21), channel_id=1, source_target_pairs={{0,2},{2,4},{4,6},{6,0},{1,3},{3,5},{5,7},{7,1},{8,10},{10,12},{12... | collective-permute-start | bytes 196616 | tf_op jit(solution)/shard_map/ppermute | solution.py:248
  56.0 2.9 %collective-permute-start.2 = (bf16[64,512]{1,0:T(8,128)(2,1)S(1)}, bf16[64,512]{1,0:T(8,128)(2,1)S(1)}, u32[]{:S(2)}, u32[]{:S(2)}) collective-permute-start(bf16[64,512]{1,0:T(8,128)(2,1)S(1)} %get-tuple-element.20), channel_id=1, source_target_pairs={{0,4},{2,6},{4,0},{6,2},{1,5},{3,7},{5,1},{7,3},{8,12},{10,14},{12... | collective-permute-start | bytes 196616 | tf_op jit(solution)/shard_map/ppermute | solution.py:248
  58.9 1.3 %collective-permute-start.3 = (bf16[64,512]{1,0:T(8,128)(2,1)S(1)}, bf16[64,512]{1,0:T(8,128)(2,1)S(1)}, u32[]{:S(2)}, u32[]{:S(2)}) collective-permute-start(bf16[64,512]{1,0:T(8,128)(2,1)S(1)} %get-tuple-element.19), channel_id=1, source_target_pairs={{0,6},{2,0},{4,2},{6,4},{1,7},{3,1},{5,3},{7,5},{8,14},{10,8},{12,... | collective-permute-start | bytes 196616 | tf_op jit(solution)/shard_map/ppermute | solution.py:248
  60.3 0.0 collective-permute-done.1.refs_4_
  60.3 2.1 %collective-permute-done.2.refs_5_ = bf16[64,512]{1,0:T(8,128)(2,1)S(1)} collective-permute-done((bf16[64,512]{1,0:T(8,128)(2,1)S(1)}, bf16[64,512]{1,0:T(8,128)(2,1)S(1)}, u32[]{:S(2)}, u32[]{:S(2)}) %collective-permute-start.2) | collective-permute-done | bytes 65568 | tf_op jit(solution)/shard_map/ppermute | solution.py:248
  62.4 0.8 collective-permute-done.3.refs_6_
  63.2 0.9 %sigma_rows.1 = (f32[64,384]{1,0:T(8,128)}, f32[64,64]{1,0:T(8,128)}, f32[64,384]{1,0:T(8,128)}, f32[1,128]{1,0:T(1,128)S(1)}) custom-call(bf16[32,32,128]{2,1,0:T(8,128)(2,1)S(1)} %all-to-all-done.1.gathered.refs_0_, f32[64,384]{1,0:T(8,128)S(1)} %dynamic-slice_bitcast_fusion.refs_1_, f32[1,384]{1,0:T(1,128)S(1)} %dynamic_slice.7.refs_2_, ...), custom_call_target="tpu_custom_call" | custom-call | flops 491520 | bytes 393216 | tf_op jit(solution)/shard_map/sigma_rows/pallas_call | solution.py:225
  64.1 0.0 collective-permute-start.4
  64.1 1.2 %collective-permute-done.4 = f32[1,128]{1,0:T(1,128)S(1)} collective-permute-done((f32[1,128]{1,0:T(1,128)S(1)}, f32[1,128]{1,0:T(1,128)S(1)}, u32[]{:S(2)}, u32[]{:S(2)}) %collective-permute-start.4) | collective-permute-done | bytes 544 | tf_op jit(solution)/shard_map/ppermute | solution.py:248
  65.3 19.9 %all_to_all.15 = f32[128,1,128]{2,1,0:T(1,128)S(1)} all-to-all(f32[128,1,128]{2,1,0:T(1,128)S(1)} %broadcast_in_dim.14), channel_id=1, replica_groups=mesh['z'=8,'x'=4,'y'=4,'c'=2] {'z','x','y'}, dimensions={0} | all-to-all | bytes 131072 | tf_op jit(solution)/shard_map/all_to_all | solution.py:243
  85.2 0.5 add_sqrt_fusion
  (13 shorter events, 0.2 us)
Async XLA Ops:
  7.4 22.8 %all-to-all-start = ((bf16[32,32,128]{2,1,0:T(8,128)(2,1)}), bf16[32,32,128]{2,1,0:T(8,128)(2,1)S(1)}, u32[]{:S(2)}, u32[]{:S(2)}) async-start(bf16[32,32,128]{2,1,0:T(8,128)(2,1)} %totals.1), calls=%async_computation | async-start | bytes 524288 | tf_op jit(solution)/shard_map/all_to_all | solution.py:243
  31.1 16.0 %all-to-all-start.1 = ((bf16[32,32,128]{2,1,0:T(8,128)(2,1)}), bf16[32,32,128]{2,1,0:T(8,128)(2,1)S(1)}, u32[]{:S(2)}, u32[]{:S(2)}) async-start(bf16[32,32,128]{2,1,0:T(8,128)(2,1)} %broadcast_in_dim.13), calls=%async_computation.1 | async-start | bytes 524288 | tf_op jit(solution)/shard_map/all_to_all | solution.py:243
  52.3 1.7 %collective-permute-start = (bf16[5,64,512]{2,1,0:T(8,128)(2,1)S(1)}, bf16[5,64,512]{2,1,0:T(8,128)(2,1)S(1)}, u32[]{:S(2)}, u32[]{:S(2)}) collective-permute-start(bf16[5,64,512]{2,1,0:T(8,128)(2,1)S(1)} %get-tuple-element.11), channel_id=1, source_target_pairs={{0,1},{1,0},{2,3},{3,2},{4,5},{5,4},{6,7},{7,6},{8,9},{9,8},{10,11... | collective-permute-start | bytes 983048 | tf_op jit(solution)/shard_map/ppermute | solution.py:248
  54.3 5.9 %collective-permute-start.1 = (bf16[64,512]{1,0:T(8,128)(2,1)S(1)}, bf16[64,512]{1,0:T(8,128)(2,1)S(1)}, u32[]{:S(2)}, u32[]{:S(2)}) collective-permute-start(bf16[64,512]{1,0:T(8,128)(2,1)S(1)} %get-tuple-element.21), channel_id=1, source_target_pairs={{0,2},{2,4},{4,6},{6,0},{1,3},{3,5},{5,7},{7,1},{8,10},{10,12},{12... | collective-permute-start | bytes 196616 | tf_op jit(solution)/shard_map/ppermute | solution.py:248
  56.0 6.4 %collective-permute-start.2 = (bf16[64,512]{1,0:T(8,128)(2,1)S(1)}, bf16[64,512]{1,0:T(8,128)(2,1)S(1)}, u32[]{:S(2)}, u32[]{:S(2)}) collective-permute-start(bf16[64,512]{1,0:T(8,128)(2,1)S(1)} %get-tuple-element.20), channel_id=1, source_target_pairs={{0,4},{2,6},{4,0},{6,2},{1,5},{3,7},{5,1},{7,3},{8,12},{10,14},{12... | collective-permute-start | bytes 196616 | tf_op jit(solution)/shard_map/ppermute | solution.py:248
  58.9 4.3 %collective-permute-start.3 = (bf16[64,512]{1,0:T(8,128)(2,1)S(1)}, bf16[64,512]{1,0:T(8,128)(2,1)S(1)}, u32[]{:S(2)}, u32[]{:S(2)}) collective-permute-start(bf16[64,512]{1,0:T(8,128)(2,1)S(1)} %get-tuple-element.19), channel_id=1, source_target_pairs={{0,6},{2,0},{4,2},{6,4},{1,7},{3,1},{5,3},{7,5},{8,14},{10,8},{12,... | collective-permute-start | bytes 196616 | tf_op jit(solution)/shard_map/ppermute | solution.py:248
  64.1 1.2 %collective-permute-start.4 = (f32[1,128]{1,0:T(1,128)S(1)}, f32[1,128]{1,0:T(1,128)S(1)}, u32[]{:S(2)}, u32[]{:S(2)}) collective-permute-start(f32[1,128]{1,0:T(1,128)S(1)} %get-tuple-element.15), channel_id=1, source_target_pairs={{0,1},{1,0},{2,3},{3,2},{4,5},{5,4},{6,7},{7,6},{8,9},{9,8},{10,11... | collective-permute-start | bytes 1544 | tf_op jit(solution)/shard_map/ppermute | solution.py:248

commit v2 on v1

--- a/solution.py
+++ b/solution.py
@@ -126,36 +126,54 @@
 
 def coupled_kernel(integrals, kept, gathered, other, own, rows, held, sems):
     ys, cs = lax.axis_size("y"), lax.axis_size("c")
-    block_rows = integrals.shape[0] // ys
-    share_rows = block_rows // cs
+    saved = kept.shape[0]
+    share_rows = integrals.shape[0] // (ys * cs)
     y, c = lax.axis_index("y"), lax.axis_index("c")
-    copies = []
-    for n in range(1, ys):
-        copies.append(pltpu.make_async_copy(integrals.at[pl.ds(n * block_rows, block_rows)], held.at[n - 1], sems.at[n - 1]))
-        copies[-1].start()
+    size = held.shape[1]
+    copies = [
+        pltpu.make_async_copy(integrals.at[pl.ds(saved + n * size, size)], held.at[n], sems.at[n])
+        for n in range(held.shape[0])
+    ]
+    for copy in copies:
+        copy.start()
     aux_rows(gathered, rows)
     a = rows[...]
     gram = lax.dot_general(a, a, NT, preferred_element_type=F32)
     high, low = split_two(jnp.concatenate([gram, gram], axis=1))
     none = jnp.zeros((a.shape[0], share_rows), F32)
-    own[ys] = jnp.concatenate([none, low], axis=1)
-    other[ys] = jnp.concatenate([none, low], axis=1).astype(BF)
+    low = jnp.concatenate([none, low], axis=1)
+    own[ys] = low
+    other[ys] = low.astype(BF)
     for n in range(ys):
-        if n:
-            copies[n - 1].wait()
-        source = held[n - 1] if n else kept[...]
+        own[n, :, share_rows:] = high
+        other[n, :, share_rows:] = high.astype(BF)
+
+    def emit(first, source):
         block = lax.dot_general(a, source, NT, preferred_element_type=F32)
-        left, right = block[:, :share_rows], block[:, share_rows:]
-        to = lax.rem(n + ys - y, ys)
-        own[to] = jnp.concatenate([jnp.where(c == 0, left, right), high], axis=1)
-        other[to] = jnp.concatenate([jnp.where(c == 0, right, left), high], axis=1).astype(BF)
+        for u in range(source.shape[0] // share_rows):
+            n, half = divmod(first // share_rows + u, cs)
+            to = lax.rem(n + ys - y, ys)
+            piece = block[:, u * share_rows : (u + 1) * share_rows]
+
+            @pl.when(c == half)
+            def _():
+                own[to, :, :share_rows] = piece
+
+            @pl.when(c != half)
+            def _():
+                other[to, :, :share_rows] = piece.astype(BF)
+
+    emit(0, kept[...])
+    for n, copy in enumerate(copies):
+        copy.wait()
+        emit(saved + n * size, held[n])
 
 
 def coupled(integrals, kept, gathered, vecs):
     pairs, aux = integrals.shape
     ys = lax.axis_size("y")
-    block_rows = pairs // ys
-    wide = block_rows // lax.axis_size("c") + 2 * vecs
+    wide = pairs // (ys * lax.axis_size("c")) + 2 * vecs
+    waits = 2
     return pl.pallas_call(
         coupled_kernel,
         out_shape=[
@@ -166,8 +184,8 @@
         out_specs=[VMEM, VMEM],
         scratch_shapes=[
             pltpu.VMEM((vecs, aux), BF),
-            pltpu.VMEM((ys - 1, block_rows, aux), BF),
-            pltpu.SemaphoreType.DMA((ys - 1,)),
+            pltpu.VMEM((waits, (pairs - kept.shape[0]) // waits, aux), BF),
+            pltpu.SemaphoreType.DMA((waits,)),
         ],
         compiler_params=pltpu.CompilerParams(vmem_limit_bytes=COUPLED_LIMIT),
         cost_estimate=pl.CostEstimate(flops=2 * pairs * aux * 256, bytes_accessed=2 * pairs * aux, transcendentals=0),
@@ -259,14 +277,17 @@
     gaps = energy_gaps.reshape(1, pairs)
     parts = totals(integrals, trial, gaps, groups)
     mine = share(exchange(parts, PAIR), per)
-    gathered = exchange(mine, PAIR)
-    other, own = coupled(integrals, lax.slice_in_dim(integrals, 0, pairs // ys, axis=0), gathered, vecs)
-    arrived = shifted(other, "c", 1)
-    mine, *sent = deal(own, arrived, vecs)
-    came = [shifted(block, "y", k + 1) for k, block in enumerate(sent)]
     first = (lax.axis_index("y") * cs + lax.axis_index("c")) * share_rows
     own_trial = lax.dynamic_slice_in_dim(trial, first, share_rows, 1)
     own_gaps = lax.dynamic_slice_in_dim(gaps, first, share_rows, 1)
+    kept = lax.slice_in_dim(integrals, 0, pairs // ys, axis=0)
+    mine, own_trial, own_gaps, kept = lax.optimization_barrier((mine, own_trial, own_gaps, kept))
+    gathered = exchange(mine, PAIR)
+    other, own = coupled(integrals, kept, gathered, vecs)
+    arrived = shifted(other, "c", 1)
+    mine, *sent = deal(own, arrived, vecs)
+    far = shifted(sent[1], "y", 2)
+    came = [shifted(sent[0], "y", 1), far, shifted(sent[2], "y", 3)]
     sigma, subspace, residuals, norms = sigma_rows(total_pairs, per, gathered, own_trial, own_gaps, [mine, *came])
     norms = norms + shifted(norms, "c", 1)
     everyone = ("z", "x", "y")

time: 86.8 us -> 85.3 us (0.983)
  blocking collectives: 19.9 us -> 35.7 us
  waiting for transfers between devices: 23.7 us -> 13.2 us
  starting transfers between devices: 23.2 us -> 17.6 us
    all_to_all x1 -> x2, blocking collectives: 19.9 us -> 35.7 us  [exchange(): return lax.all_to_all(value, axis, 0, 0, tiled=True)]
    all_to_all x2 -> x1, waiting for transfers between devices: 19 us -> 7.61 us  [exchange(): return lax.all_to_all(value, axis, 0, 0, tiled=True)]
    all_to_all x2 -> x1, starting transfers between devices: 17.2 us -> 11.6 us  [exchange(): return lax.all_to_all(value, axis, 0, 0, tiled=True)]
    ppermute x5, waiting for transfers between devices: 4.73 us -> 5.64 us  [shifted(): return lax.ppermute(value, axis, [(i, (i + by) % n) for i in range(n)])]
  transfers between devices with their start and end apart: 7 -> 6, of which waited for: 6 -> 5; matrix products, arithmetic and copies ran while one was open for 4% -> 4% of each run, Pallas kernels for 0% -> 0%
where the time goes in v2:
time: 85.3 us; the launch traced here: 84.3 us
  blocking collectives  35.7 us (42%)
  starting transfers between devices  17.6 us (21%)
  waiting for transfers between devices  13.2 us (15%)
  Pallas kernels  12.3 us (14%)
  local copies, waits for them, and re-layouts  3.69 us (4%)
  other arithmetic  0.98 us (1%)
    all_to_all x2, blocking collectives, exchange(): return lax.all_to_all(value, axis, 0, 0, tiled=True)  35.7 us
    all_to_all x1, starting transfers between devices, exchange(): return lax.all_to_all(value, axis, 0, 0, tiled=True)  11.6 us
    all_to_all x1, waiting for transfers between devices, exchange(): return lax.all_to_all(value, axis, 0, 0, tiled=True)  7.61 us
    pallas_call x1, Pallas kernels, totals(): pl.pallas_call(lambda *refs: totals_kernel(groups, *refs), out_shape=jax....  6.73 us
    ppermute x5, starting transfers between devices, shifted(): return lax.ppermute(value, axis, [(i, (i + by) % n) for i in range(n)])  6 us
    ppermute x5, waiting for transfers between devices, shifted(): return lax.ppermute(value, axis, [(i, (i + by) % n) for i in range(n)])  5.64 us
    pallas_call x1, Pallas kernels, coupled(): pl.pallas_call(coupled_kernel, out_shape=[jax.ShapeDtypeStruct((ys + 1, v...  4.66 us
    slice x1, local copies, waits for them, and re-layouts, local(): kept = lax.slice_in_dim(integrals, 0, pairs // ys, axis=0)  1.82 us
  transfers between devices with their start and end apart: 6, of which 5 were waited for; matrix products, arithmetic and copies ran while one was open for 4% of the time, Pallas kernels for 0%

profile of v2, /device:TPU:2, one launch (start us, length us, event | category | flops | bytes accessed | tf_op | source)
XLA Modules:
  0.0 84.3 jit_solution(2419411730407900771)
XLA Ops:
  0.6 6.7 %totals.1 = bf16[32,32,128]{2,1,0:T(8,128)(2,1)} custom-call(bf16[3072,1536]{1,0:T(8,128)(2,1)} %integrals.1, f32[64,3072]{1,0:T(8,128)} %bitcast.25, f32[1,3072]{1,0:T(1,128)} %bitcast.27), custom_call_target="tpu_custom_call" | custom-call | flops 2415919104 | bytes 9437184 | tf_op jit(solution)/shard_map/totals/pallas_call | solution.py:86
  7.4 11.6 %all-to-all-start = ((bf16[32,32,128]{2,1,0:T(8,128)(2,1)}), bf16[32,32,128]{2,1,0:T(8,128)(2,1)S(1)}, u32[]{:S(2)}, u32[]{:S(2)}) async-start(bf16[32,32,128]{2,1,0:T(8,128)(2,1)} %totals.1), calls=%async_computation | async-start | bytes 524288 | tf_op jit(solution)/shard_map/all_to_all | solution.py:261
  19.0 1.8 %slice.44.kept = bf16[768,1536]{1,0:T(8,128)(2,1)S(1)} slice(bf16[3072,1536]{1,0:T(8,128)(2,1)} %integrals.1), slice={[0:768], [0:1536]} | slice | bytes 4718592 | tf_op jit(solution)/shard_map/slice | solution.py:283
  20.8 0.8 dynamic-slice.7
  21.6 0.1 pad.3.clone
  21.7 0.9 %dynamic-slice_bitcast_fusion.refs_1_ = f32[64,384]{1,0:T(8,128)S(1)} fusion(f32[3072,64]{0,1:T(8,128)} %param.5, s32[]{:T(128)S(6)} %select_n.12), kind=kLoop, calls=%fused_computation.10 | loop fusion | bytes 196612 | tf_op jit(solution)/shard_map/dynamic_slice | solution.py:281
  22.6 7.6 %all-to-all-done = bf16[32,32,128]{2,1,0:T(8,128)(2,1)S(1)} async-done(((bf16[32,32,128]{2,1,0:T(8,128)(2,1)}), bf16[32,32,128]{2,1,0:T(8,128)(2,1)S(1)}, u32[]{:S(2)}, u32[]{:S(2)}) %all-to-all-start) | async-done | bytes 262176 | tf_op jit(solution)/shard_map/all_to_all | solution.py:261
  30.3 0.1 maximum_maximum_fusion
  30.4 15.8 %all_to_all.15.gathered.refs_0_ = bf16[32,32,128]{2,1,0:T(8,128)(2,1)S(1)} all-to-all(bf16[32,32,128]{2,1,0:T(8,128)(2,1)S(1)} %broadcast_in_dim.13), channel_id=1, replica_groups=mesh['z'=8,'x'=4,'y'=4,'c'=2] {'z','x'}, dimensions={0} | all-to-all | bytes 524288 | tf_op jit(solution)/shard_map/all_to_all | solution.py:261
  46.2 4.7 %coupled.1 = (bf16[5,64,512]{2,1,0:T(8,128)(2,1)S(1)}, f32[5,64,512]{2,1,0:T(8,128)S(1)}) custom-call(bf16[3072,1536]{1,0:T(8,128)(2,1)} %integrals.1, bf16[768,1536]{1,0:T(8,128)(2,1)S(1)} %slice.44.kept, bf16[32,32,128]{2,1,0:T(8,128)(2,1)S(1)} %all_to_all.15.gathered.refs_0_), custom_call_target="tpu_custom_call" | custom-call | flops 2415919104 | bytes 9437184 | tf_op jit(solution)/shard_map/coupled/pallas_call | solution.py:177
  50.9 0.1 collective-permute-start
  51.0 1.6 %collective-permute-done = bf16[5,64,512]{2,1,0:T(8,128)(2,1)S(1)} collective-permute-done((bf16[5,64,512]{2,1,0:T(8,128)(2,1)S(1)}, bf16[5,64,512]{2,1,0:T(8,128)(2,1)S(1)}, u32[]{:S(2)}, u32[]{:S(2)}) %collective-permute-start) | collective-permute-done | bytes 327712 | tf_op jit(solution)/shard_map/ppermute | solution.py:266
  52.6 0.1 convert_add_fusion
  52.7 0.2 fusion.3
  52.9 1.7 %collective-permute-start.1 = (bf16[64,512]{1,0:T(8,128)(2,1)S(1)}, bf16[64,512]{1,0:T(8,128)(2,1)S(1)}, u32[]{:S(2)}, u32[]{:S(2)}) collective-permute-start(bf16[64,512]{1,0:T(8,128)(2,1)S(1)} %get-tuple-element.29), channel_id=1, source_target_pairs={{0,2},{2,4},{4,6},{6,0},{1,3},{3,5},{5,7},{7,1},{8,10},{10,12},{12... | collective-permute-start | bytes 196616 | tf_op jit(solution)/shard_map/ppermute | solution.py:266
  54.6 2.9 %collective-permute-start.2 = (bf16[64,512]{1,0:T(8,128)(2,1)S(1)}, bf16[64,512]{1,0:T(8,128)(2,1)S(1)}, u32[]{:S(2)}, u32[]{:S(2)}) collective-permute-start(bf16[64,512]{1,0:T(8,128)(2,1)S(1)} %get-tuple-element.28), channel_id=1, source_target_pairs={{0,4},{2,6},{4,0},{6,2},{1,5},{3,7},{5,1},{7,3},{8,12},{10,14},{12... | collective-permute-start | bytes 196616 | tf_op jit(solution)/shard_map/ppermute | solution.py:266
  57.5 1.3 %collective-permute-start.3 = (bf16[64,512]{1,0:T(8,128)(2,1)S(1)}, bf16[64,512]{1,0:T(8,128)(2,1)S(1)}, u32[]{:S(2)}, u32[]{:S(2)}) collective-permute-start(bf16[64,512]{1,0:T(8,128)(2,1)S(1)} %get-tuple-element.27), channel_id=1, source_target_pairs={{0,6},{2,0},{4,2},{6,4},{1,7},{3,1},{5,3},{7,5},{8,14},{10,8},{12,... | collective-permute-start | bytes 196616 | tf_op jit(solution)/shard_map/ppermute | solution.py:266
  58.8 0.0 collective-permute-done.1.refs_4_
  58.9 2.1 %collective-permute-done.2.refs_5_ = bf16[64,512]{1,0:T(8,128)(2,1)S(1)} collective-permute-done((bf16[64,512]{1,0:T(8,128)(2,1)S(1)}, bf16[64,512]{1,0:T(8,128)(2,1)S(1)}, u32[]{:S(2)}, u32[]{:S(2)}) %collective-permute-start.2) | collective-permute-done | bytes 65568 | tf_op jit(solution)/shard_map/ppermute | solution.py:266
  61.0 0.8 collective-permute-done.3.refs_6_
  61.7 0.9 %sigma_rows.1 = (f32[64,384]{1,0:T(8,128)}, f32[64,64]{1,0:T(8,128)}, f32[64,384]{1,0:T(8,128)}, f32[1,128]{1,0:T(1,128)S(1)}) custom-call(bf16[32,32,128]{2,1,0:T(8,128)(2,1)S(1)} %all_to_all.15.gathered.refs_0_, f32[64,384]{1,0:T(8,128)S(1)} %dynamic-slice_bitcast_fusion.refs_1_, f32[1,384]{1,0:T(1,128)S(1)} %dynamic_slice.7.refs_2_, ...), custom_call_target="tpu_custom_call" | custom-call | flops 491520 | bytes 393216 | tf_op jit(solution)/shard_map/sigma_rows/pallas_call | solution.py:243
  62.7 0.0 collective-permute-start.4
  62.7 1.2 %collective-permute-done.4 = f32[1,128]{1,0:T(1,128)S(1)} collective-permute-done((f32[1,128]{1,0:T(1,128)S(1)}, f32[1,128]{1,0:T(1,128)S(1)}, u32[]{:S(2)}, u32[]{:S(2)}) %collective-permute-start.4) | collective-permute-done | bytes 544 | tf_op jit(solution)/shard_map/ppermute | solution.py:266
  63.9 19.9 %all_to_all.16 = f32[128,1,128]{2,1,0:T(1,128)S(1)} all-to-all(f32[128,1,128]{2,1,0:T(1,128)S(1)} %broadcast_in_dim.14), channel_id=1, replica_groups=mesh['z'=8,'x'=4,'y'=4,'c'=2] {'z','x','y'}, dimensions={0} | all-to-all | bytes 131072 | tf_op jit(solution)/shard_map/all_to_all | solution.py:261
  83.8 0.5 add_sqrt_fusion
  (14 shorter events, 0.2 us)
Async XLA Ops:
  7.4 22.8 %all-to-all-start = ((bf16[32,32,128]{2,1,0:T(8,128)(2,1)}), bf16[32,32,128]{2,1,0:T(8,128)(2,1)S(1)}, u32[]{:S(2)}, u32[]{:S(2)}) async-start(bf16[32,32,128]{2,1,0:T(8,128)(2,1)} %totals.1), calls=%async_computation | async-start | bytes 524288 | tf_op jit(solution)/shard_map/all_to_all | solution.py:261
  50.9 1.7 %collective-permute-start = (bf16[5,64,512]{2,1,0:T(8,128)(2,1)S(1)}, bf16[5,64,512]{2,1,0:T(8,128)(2,1)S(1)}, u32[]{:S(2)}, u32[]{:S(2)}) collective-permute-start(bf16[5,64,512]{2,1,0:T(8,128)(2,1)S(1)} %get-tuple-element.19), channel_id=1, source_target_pairs={{0,1},{1,0},{2,3},{3,2},{4,5},{5,4},{6,7},{7,6},{8,9},{9,8},{10,11... | collective-permute-start | bytes 983048 | tf_op jit(solution)/shard_map/ppermute | solution.py:266
  52.9 5.9 %collective-permute-start.1 = (bf16[64,512]{1,0:T(8,128)(2,1)S(1)}, bf16[64,512]{1,0:T(8,128)(2,1)S(1)}, u32[]{:S(2)}, u32[]{:S(2)}) collective-permute-start(bf16[64,512]{1,0:T(8,128)(2,1)S(1)} %get-tuple-element.29), channel_id=1, source_target_pairs={{0,2},{2,4},{4,6},{6,0},{1,3},{3,5},{5,7},{7,1},{8,10},{10,12},{12... | collective-permute-start | bytes 196616 | tf_op jit(solution)/shard_map/ppermute | solution.py:266
  54.6 6.4 %collective-permute-start.2 = (bf16[64,512]{1,0:T(8,128)(2,1)S(1)}, bf16[64,512]{1,0:T(8,128)(2,1)S(1)}, u32[]{:S(2)}, u32[]{:S(2)}) collective-permute-start(bf16[64,512]{1,0:T(8,128)(2,1)S(1)} %get-tuple-element.28), channel_id=1, source_target_pairs={{0,4},{2,6},{4,0},{6,2},{1,5},{3,7},{5,1},{7,3},{8,12},{10,14},{12... | collective-permute-start | bytes 196616 | tf_op jit(solution)/shard_map/ppermute | solution.py:266
  57.5 4.3 %collective-permute-start.3 = (bf16[64,512]{1,0:T(8,128)(2,1)S(1)}, bf16[64,512]{1,0:T(8,128)(2,1)S(1)}, u32[]{:S(2)}, u32[]{:S(2)}) collective-permute-start(bf16[64,512]{1,0:T(8,128)(2,1)S(1)} %get-tuple-element.27), channel_id=1, source_target_pairs={{0,6},{2,0},{4,2},{6,4},{1,7},{3,1},{5,3},{7,5},{8,14},{10,8},{12,... | collective-permute-start | bytes 196616 | tf_op jit(solution)/shard_map/ppermute | solution.py:266
  62.7 1.2 %collective-permute-start.4 = (f32[1,128]{1,0:T(1,128)S(1)}, f32[1,128]{1,0:T(1,128)S(1)}, u32[]{:S(2)}, u32[]{:S(2)}) collective-permute-start(f32[1,128]{1,0:T(1,128)S(1)} %get-tuple-element.23), channel_id=1, source_target_pairs={{0,1},{1,0},{2,3},{3,2},{4,5},{5,4},{6,7},{7,6},{8,9},{9,8},{10,11... | collective-permute-start | bytes 1544 | tf_op jit(solution)/shard_map/ppermute | solution.py:266

commit v3 on v2

--- a/solution.py
+++ b/solution.py
@@ -16,8 +16,9 @@
 NT = (((1,), (1,)), ((), ()))
 VMEM = pl.BlockSpec(memory_space=pltpu.VMEM)
 HBM = pl.BlockSpec(memory_space=pltpu.HBM)
-CHUNKS = 12
-FLIGHT = 6
+CHUNKS = 6
+FIRST = 2
+FLIGHT = 4
 TOTALS_LIMIT = 60 * 1024 * 1024
 COUPLED_LIMIT = 46 << 20
 
@@ -38,22 +39,29 @@
     gap_copy = pltpu.make_async_copy(gaps, gap_ref, small.at[1])
     x_copy.start()
     gap_copy.start()
-    for n in range(FLIGHT):
+    for n in range(FIRST):
         copy(n).start()
     x_copy.wait()
     gap_copy.wait()
-    x = x_ref[...]
-    gx = x * gap_ref[...]
-    x_high, x_low = split_two(x)
-    g_high, g_low = split_two(gx)
-    half = x_high.astype(BF)
-    low = x_low.astype(BF)
-    left = jnp.concatenate([half, low], axis=0)
-    right = jnp.concatenate([g_high.astype(BF), g_low.astype(BF)], axis=0)
-    both = lax.dot_general(left, right, NT, preferred_element_type=F32)
-    vecs = x.shape[0]
+    for n in range(FIRST, FLIGHT):
+        copy(n).start()
+    vecs = trial.shape[0]
+    total = both = squares = None
+    for n in range(CHUNKS):
+        x = x_ref[:, n * rows : (n + 1) * rows]
+        x_high, x_low = split_two(x)
+        g_high, g_low = split_two(x * gap_ref[:, n * rows : (n + 1) * rows])
+        half = x_high.astype(BF)
+        left = jnp.concatenate([half, x_low.astype(BF)], axis=0)
+        right = jnp.concatenate([g_high.astype(BF), g_low.astype(BF)], axis=0)
+        pieces = lax.dot_general(left, right, NT, preferred_element_type=F32)
+        square = jnp.sum(x * x, axis=1, keepdims=True)
+        copy(n).wait()
+        if n + FLIGHT < CHUNKS:
+            copy(n + FLIGHT).start()
+        part = jnp.dot(half, held[n * rows : (n + 1) * rows, :], preferred_element_type=F32)
+        total, both, squares = (part, pieces, square) if n == 0 else (total + part, both + pieces, squares + square)
     gram = both[:vecs, :vecs] + both[:vecs, vecs:] + both[vecs:, :vecs]
-    squares = jnp.sum(x * x, axis=1, keepdims=True)
     wide = jnp.concatenate([gram, jnp.broadcast_to(squares, (vecs, vecs))], axis=1)
     high, low_part = split_two(wide)
     per = vecs // groups
@@ -61,14 +69,6 @@
     for j in range(groups):
         stats[j, 0:per, :] = high[j * per : (j + 1) * per]
         stats[j, per : 2 * per, :] = low_part[j * per : (j + 1) * per]
-    total = None
-    for n in range(CHUNKS):
-        copy(n).wait()
-        if n + FLIGHT < CHUNKS:
-            copy(n + FLIGHT).start()
-        block = held[n * rows : (n + 1) * rows, :]
-        part = jnp.dot(half[:, n * rows : (n + 1) * rows], block, preferred_element_type=F32)
-        total = part if total is None else total + part
     columns = aux // 128
     tiles = (vecs // 8) * columns
     each = tiles // groups
@@ -138,15 +138,14 @@
         copy.start()
     aux_rows(gathered, rows)
     a = rows[...]
+    vecs = a.shape[0]
     gram = lax.dot_general(a, a, NT, preferred_element_type=F32)
-    high, low = split_two(jnp.concatenate([gram, gram], axis=1))
-    none = jnp.zeros((a.shape[0], share_rows), F32)
-    low = jnp.concatenate([none, low], axis=1)
-    own[ys] = low
-    other[ys] = low.astype(BF)
+    half = vecs // 2
+    corner = jnp.concatenate([gram[:half], gram[half:, half:]], axis=1)
+    strip = jnp.concatenate([corner[8 * i : 8 * i + 8] for i in range(half // 8)], axis=1).astype(BF)
     for n in range(ys):
-        own[n, :, share_rows:] = high
-        other[n, :, share_rows:] = high.astype(BF)
+        own[n, vecs:, :] = strip.astype(F32)
+        other[n, vecs:, :] = strip
 
     def emit(first, source):
         block = lax.dot_general(a, source, NT, preferred_element_type=F32)
@@ -157,11 +156,11 @@
 
             @pl.when(c == half)
             def _():
-                own[to, :, :share_rows] = piece
+                own[to, :vecs, :] = piece
 
             @pl.when(c != half)
             def _():
-                other[to, :, :share_rows] = piece.astype(BF)
+                other[to, :vecs, :] = piece.astype(BF)
 
     emit(0, kept[...])
     for n, copy in enumerate(copies):
@@ -172,13 +171,13 @@
 def coupled(integrals, kept, gathered, vecs):
     pairs, aux = integrals.shape
     ys = lax.axis_size("y")
-    wide = pairs // (ys * lax.axis_size("c")) + 2 * vecs
+    shape = (ys, vecs + 8, pairs // (ys * lax.axis_size("c")))
     waits = 2
     return pl.pallas_call(
         coupled_kernel,
         out_shape=[
-            jax.ShapeDtypeStruct((ys + 1, vecs, wide), BF),
-            jax.ShapeDtypeStruct((ys + 1, vecs, wide), F32),
+            jax.ShapeDtypeStruct(shape, BF),
+            jax.ShapeDtypeStruct(shape, F32),
         ],
         in_specs=[HBM, VMEM, VMEM],
         out_specs=[VMEM, VMEM],
@@ -193,29 +192,27 @@
     )(integrals, kept, gathered)
 
 
-def deal(own, other, vecs):
-    ys, wide = own.shape[0] - 1, own.shape[2]
+def deal(own, other):
     total = own + other.astype(F32)
-    total = total[:ys] + total[ys:]
-    lane = lax.broadcasted_iota(jnp.int32, total.shape, 2)
-    high = lax.reduce_precision(total, 8, 7)
-    low = lax.reduce_precision(total - high, 8, 7)
-    parts = jnp.where(lane < wide - vecs, high, low)
-    mine = jnp.where(lane[0] < wide - 2 * vecs, total[0], parts[0])
-    return mine, *[parts[k].astype(BF) for k in range(1, ys)]
+    return total[0], *[total[k].astype(BF) for k in range(1, own.shape[0])]
 
 
 def sigma_kernel(total_pairs, per, gathered, trial, gaps, kept, one, two, three, sigma, subspace, residuals, norms, grams):
     ys = 4
     y = lax.axis_index("y")
     vecs, rows = trial.shape
-    block = kept[:, :rows]
+    block = kept[:vecs, :]
     for part in (one, two, three):
-        block = block + part[:, :rows].astype(F32)
+        block = block + part[:vecs, :].astype(F32)
     for k, part in enumerate((kept, one, two, three)):
-        grams[lax.rem(y + ys - k, ys)] = part[:, rows:].astype(F32)
-    gram = grams[0] + grams[1] + grams[2] + grams[3]
-    gram = gram[:, :vecs] + gram[:, vecs:]
+        grams[lax.rem(y + ys - k, ys)] = part[vecs:, :].astype(BF).astype(F32)
+    strip = grams[0] + grams[1] + grams[2] + grams[3]
+    half = vecs // 2
+    lanes = half + vecs
+    corner = jnp.concatenate([strip[:, lanes * i : lanes * i + lanes] for i in range(half // 8)], axis=0)
+    turned = jnp.transpose(jnp.concatenate([corner, jnp.zeros((half, 128 - lanes), F32)], axis=1))
+    lower = jnp.concatenate([turned[half:vecs], corner[:, vecs:]], axis=1)
+    gram = jnp.concatenate([corner[:, :vecs], lower], axis=0)
     groups, tall, _ = gathered.shape
     base = tall - 8
     wide = jnp.concatenate(
@@ -250,7 +247,7 @@
         ],
         in_specs=[VMEM] * 7,
         out_specs=[VMEM] * 4,
-        scratch_shapes=[pltpu.VMEM((4, vecs, 128), F32)],
+        scratch_shapes=[pltpu.VMEM((4, 8, rows), F32)],
         compiler_params=pltpu.CompilerParams(vmem_limit_bytes=16 << 20),
         cost_estimate=pl.CostEstimate(flops=20 * trial.size, bytes_accessed=16 * trial.size, transcendentals=0),
         name="sigma_rows",
@@ -285,7 +282,7 @@
     gathered = exchange(mine, PAIR)
     other, own = coupled(integrals, kept, gathered, vecs)
     arrived = shifted(other, "c", 1)
-    mine, *sent = deal(own, arrived, vecs)
+    mine, *sent = deal(own, arrived)
     far = shifted(sent[1], "y", 2)
     came = [shifted(sent[0], "y", 1), far, shifted(sent[2], "y", 3)]
     sigma, subspace, residuals, norms = sigma_rows(total_pairs, per, gathered, own_trial, own_gaps, [mine, *came])

time: 85.3 us -> 83.2 us (0.975)
  waiting for transfers between devices: 13.2 us -> 14.9 us
  blocking collectives: 35.7 us -> 34.5 us
  starting transfers between devices: 17.6 us -> 16.4 us
  Pallas kernels: 12.3 us -> 11.2 us
    ppermute x5, waiting for transfers between devices: 5.64 us -> 7.33 us  [shifted(): return lax.ppermute(value, axis, [(i, (i + by) % n) for i in range(n)])]
    ppermute x5, starting transfers between devices: 6 us -> 4.78 us  [shifted(): return lax.ppermute(value, axis, [(i, (i + by) % n) for i in range(n)])]
    all_to_all x2, blocking collectives: 35.7 us -> 34.5 us  [exchange(): return lax.all_to_all(value, axis, 0, 0, tiled=True)]
    pallas_call x1, Pallas kernels: 6.73 us -> 5.58 us  [totals(): pl.pallas_call(lambda *refs: totals_kernel(groups, *refs), out_shape=jax....]
  transfers between devices with their start and end apart: 6 -> 6, of which waited for: 5 -> 6; matrix products, arithmetic and copies ran while one was open for 4% -> 4% of each run, Pallas kernels for 0% -> 0%
where the time goes in v3:
time: 83.2 us; the launch traced here: 82.3 us
  blocking collectives  34.5 us (41%)
  starting transfers between devices  16.4 us (20%)
  waiting for transfers between devices  14.9 us (18%)
  Pallas kernels  11.2 us (13%)
  local copies, waits for them, and re-layouts  3.69 us (4%)
    all_to_all x2, blocking collectives, exchange(): return lax.all_to_all(value, axis, 0, 0, tiled=True)  34.5 us
    all_to_all x1, starting transfers between devices, exchange(): return lax.all_to_all(value, axis, 0, 0, tiled=True)  11.6 us
    all_to_all x1, waiting for transfers between devices, exchange(): return lax.all_to_all(value, axis, 0, 0, tiled=True)  7.61 us
    ppermute x5, waiting for transfers between devices, shifted(): return lax.ppermute(value, axis, [(i, (i + by) % n) for i in range(n)])  7.33 us
    pallas_call x1, Pallas kernels, totals(): pl.pallas_call(lambda *refs: totals_kernel(groups, *refs), out_shape=jax....  5.58 us
    ppermute x5, starting transfers between devices, shifted(): return lax.ppermute(value, axis, [(i, (i + by) % n) for i in range(n)])  4.78 us
    pallas_call x1, Pallas kernels, coupled(): pl.pallas_call(coupled_kernel, out_shape=[jax.ShapeDtypeStruct(shape, BF)...  4.63 us
    slice x1, local copies, waits for them, and re-layouts, local(): kept = lax.slice_in_dim(integrals, 0, pairs // ys, axis=0)  1.82 us
  transfers between devices with their start and end apart: 6, of which 6 were waited for; matrix products, arithmetic and copies ran while one was open for 4% of the time, Pallas kernels for 0%

profile of v3, /device:TPU:2, one launch (start us, length us, event | category | flops | bytes accessed | tf_op | source)
XLA Modules:
  0.0 82.3 jit_solution(14011336536468339039)
XLA Ops:
  0.6 5.6 %totals.1 = bf16[32,32,128]{2,1,0:T(8,128)(2,1)} custom-call(bf16[3072,1536]{1,0:T(8,128)(2,1)} %integrals.1, f32[64,3072]{1,0:T(8,128)} %bitcast.17, f32[1,3072]{1,0:T(1,128)} %bitcast.19), custom_call_target="tpu_custom_call" | custom-call | flops 2415919104 | bytes 9437184 | tf_op jit(solution)/shard_map/totals/pallas_call | solution.py:86
  6.2 11.6 %all-to-all-start = ((bf16[32,32,128]{2,1,0:T(8,128)(2,1)}), bf16[32,32,128]{2,1,0:T(8,128)(2,1)S(1)}, u32[]{:S(2)}, u32[]{:S(2)}) async-start(bf16[32,32,128]{2,1,0:T(8,128)(2,1)} %totals.1), calls=%async_computation | async-start | bytes 524288 | tf_op jit(solution)/shard_map/all_to_all | solution.py:258
  17.9 1.8 %slice.34.kept = bf16[768,1536]{1,0:T(8,128)(2,1)S(1)} slice(bf16[3072,1536]{1,0:T(8,128)(2,1)} %integrals.1), slice={[0:768], [0:1536]} | slice | bytes 4718592 | tf_op jit(solution)/shard_map/slice | solution.py:280
  19.7 0.8 dynamic-slice.7
  20.5 0.1 pad.3.clone
  20.6 0.9 %dynamic-slice_bitcast_fusion.refs_1_ = f32[64,384]{1,0:T(8,128)S(1)} fusion(f32[3072,64]{0,1:T(8,128)} %param.5, s32[]{:T(128)S(6)} %select_n.4), kind=kLoop, calls=%fused_computation.3 | loop fusion | bytes 196612 | tf_op jit(solution)/shard_map/dynamic_slice | solution.py:278
  21.5 7.6 %all-to-all-done = bf16[32,32,128]{2,1,0:T(8,128)(2,1)S(1)} async-done(((bf16[32,32,128]{2,1,0:T(8,128)(2,1)}), bf16[32,32,128]{2,1,0:T(8,128)(2,1)S(1)}, u32[]{:S(2)}, u32[]{:S(2)}) %all-to-all-start) | async-done | bytes 262176 | tf_op jit(solution)/shard_map/all_to_all | solution.py:258
  29.1 0.1 maximum_maximum_fusion
  29.3 15.8 %all_to_all.15.gathered.refs_0_ = bf16[32,32,128]{2,1,0:T(8,128)(2,1)S(1)} all-to-all(bf16[32,32,128]{2,1,0:T(8,128)(2,1)S(1)} %broadcast_in_dim.13), channel_id=1, replica_groups=mesh['z'=8,'x'=4,'y'=4,'c'=2] {'z','x'}, dimensions={0} | all-to-all | bytes 524288 | tf_op jit(solution)/shard_map/all_to_all | solution.py:258
  45.1 4.6 %coupled.1 = (bf16[4,72,384]{2,1,0:T(8,128)(2,1)S(1)}, f32[4,72,384]{2,1,0:T(8,128)S(1)}) custom-call(bf16[3072,1536]{1,0:T(8,128)(2,1)} %integrals.1, bf16[768,1536]{1,0:T(8,128)(2,1)S(1)} %slice.34.kept, bf16[32,32,128]{2,1,0:T(8,128)(2,1)S(1)} %all_to_all.15.gathered.refs_0_), custom_call_target="tpu_custom_call" | custom-call | flops 2415919104 | bytes 9437184 | tf_op jit(solution)/shard_map/coupled/pallas_call | solution.py:176
  49.7 0.1 collective-permute-start
  49.8 1.5 %collective-permute-done = bf16[4,72,384]{2,1,0:T(8,128)(2,1)S(1)} collective-permute-done((bf16[4,72,384]{2,1,0:T(8,128)(2,1)S(1)}, bf16[4,72,384]{2,1,0:T(8,128)(2,1)S(1)}, u32[]{:S(2)}, u32[]{:S(2)}) %collective-permute-start) | collective-permute-done | bytes 221216 | tf_op jit(solution)/shard_map/ppermute | solution.py:263
  51.3 0.1 fusion.1
  51.4 3.1 %collective-permute-start.3 = (bf16[72,384]{1,0:T(8,128)(2,1)S(1)}, bf16[72,384]{1,0:T(8,128)(2,1)S(1)}, u32[]{:S(2)}, u32[]{:S(2)}) collective-permute-start(bf16[72,384]{1,0:T(8,128)(2,1)S(1)} %get-tuple-element.26), channel_id=1, source_target_pairs={{0,6},{2,0},{4,2},{6,4},{1,7},{3,1},{5,3},{7,5},{8,14},{10,8},{12,... | collective-permute-start | bytes 165896 | tf_op jit(solution)/shard_map/ppermute | solution.py:263
  54.5 0.6 collective-permute-start.2
  55.1 1.0 %collective-permute-start.1 = (bf16[72,384]{1,0:T(8,128)(2,1)S(1)}, bf16[72,384]{1,0:T(8,128)(2,1)S(1)}, u32[]{:S(2)}, u32[]{:S(2)}) collective-permute-start(bf16[72,384]{1,0:T(8,128)(2,1)S(1)} %get-tuple-element.28), channel_id=1, source_target_pairs={{0,2},{2,4},{4,6},{6,0},{1,3},{3,5},{5,7},{7,1},{8,10},{10,12},{12... | collective-permute-start | bytes 165896 | tf_op jit(solution)/shard_map/ppermute | solution.py:263
  56.1 0.6 collective-permute-done.3.refs_6_
  56.7 3.5 %collective-permute-done.2.refs_5_ = bf16[72,384]{1,0:T(8,128)(2,1)S(1)} collective-permute-done((bf16[72,384]{1,0:T(8,128)(2,1)S(1)}, bf16[72,384]{1,0:T(8,128)(2,1)S(1)}, u32[]{:S(2)}, u32[]{:S(2)}) %collective-permute-start.2) | collective-permute-done | bytes 55328 | tf_op jit(solution)/shard_map/ppermute | solution.py:263
  60.2 0.6 collective-permute-done.1.refs_4_
  60.8 1.0 %sigma_rows.1 = (f32[64,384]{1,0:T(8,128)}, f32[64,64]{1,0:T(8,128)}, f32[64,384]{1,0:T(8,128)}, f32[1,128]{1,0:T(1,128)S(1)}) custom-call(bf16[32,32,128]{2,1,0:T(8,128)(2,1)S(1)} %all_to_all.15.gathered.refs_0_, f32[64,384]{1,0:T(8,128)S(1)} %dynamic-slice_bitcast_fusion.refs_1_, f32[1,384]{1,0:T(1,128)S(1)} %dynamic_slice.7.refs_2_, ...), custom_call_target="tpu_custom_call" | custom-call | flops 491520 | bytes 393216 | tf_op jit(solution)/shard_map/sigma_rows/pallas_call | solution.py:240
  61.8 0.0 collective-permute-start.4
  61.8 1.2 %collective-permute-done.4 = f32[1,128]{1,0:T(1,128)S(1)} collective-permute-done((f32[1,128]{1,0:T(1,128)S(1)}, f32[1,128]{1,0:T(1,128)S(1)}, u32[]{:S(2)}, u32[]{:S(2)}) %collective-permute-start.4) | collective-permute-done | bytes 544 | tf_op jit(solution)/shard_map/ppermute | solution.py:263
  63.0 18.7 %all_to_all.16 = f32[128,1,128]{2,1,0:T(1,128)S(1)} all-to-all(f32[128,1,128]{2,1,0:T(1,128)S(1)} %broadcast_in_dim.14), channel_id=1, replica_groups=mesh['z'=8,'x'=4,'y'=4,'c'=2] {'z','x','y'}, dimensions={0} | all-to-all | bytes 131072 | tf_op jit(solution)/shard_map/all_to_all | solution.py:258
  81.7 0.5 add_sqrt_fusion
  (11 shorter events, 0.2 us)
Async XLA Ops:
  6.2 22.8 %all-to-all-start = ((bf16[32,32,128]{2,1,0:T(8,128)(2,1)}), bf16[32,32,128]{2,1,0:T(8,128)(2,1)S(1)}, u32[]{:S(2)}, u32[]{:S(2)}) async-start(bf16[32,32,128]{2,1,0:T(8,128)(2,1)} %totals.1), calls=%async_computation | async-start | bytes 524288 | tf_op jit(solution)/shard_map/all_to_all | solution.py:258
  49.7 1.6 %collective-permute-start = (bf16[4,72,384]{2,1,0:T(8,128)(2,1)S(1)}, bf16[4,72,384]{2,1,0:T(8,128)(2,1)S(1)}, u32[]{:S(2)}, u32[]{:S(2)}) collective-permute-start(bf16[4,72,384]{2,1,0:T(8,128)(2,1)S(1)} %get-tuple-element.19), channel_id=1, source_target_pairs={{0,1},{1,0},{2,3},{3,2},{4,5},{5,4},{6,7},{7,6},{8,9},{9,8},{10,11... | collective-permute-start | bytes 663560 | tf_op jit(solution)/shard_map/ppermute | solution.py:263
  51.4 5.3 %collective-permute-start.3 = (bf16[72,384]{1,0:T(8,128)(2,1)S(1)}, bf16[72,384]{1,0:T(8,128)(2,1)S(1)}, u32[]{:S(2)}, u32[]{:S(2)}) collective-permute-start(bf16[72,384]{1,0:T(8,128)(2,1)S(1)} %get-tuple-element.26), channel_id=1, source_target_pairs={{0,6},{2,0},{4,2},{6,4},{1,7},{3,1},{5,3},{7,5},{8,14},{10,8},{12,... | collective-permute-start | bytes 165896 | tf_op jit(solution)/shard_map/ppermute | solution.py:263
  54.5 5.7 %collective-permute-start.2 = (bf16[72,384]{1,0:T(8,128)(2,1)S(1)}, bf16[72,384]{1,0:T(8,128)(2,1)S(1)}, u32[]{:S(2)}, u32[]{:S(2)}) collective-permute-start(bf16[72,384]{1,0:T(8,128)(2,1)S(1)} %get-tuple-element.27), channel_id=1, source_target_pairs={{0,4},{2,6},{4,0},{6,2},{1,5},{3,7},{5,1},{7,3},{8,12},{10,14},{12... | collective-permute-start | bytes 165896 | tf_op jit(solution)/shard_map/ppermute | solution.py:263
  55.1 5.7 %collective-permute-start.1 = (bf16[72,384]{1,0:T(8,128)(2,1)S(1)}, bf16[72,384]{1,0:T(8,128)(2,1)S(1)}, u32[]{:S(2)}, u32[]{:S(2)}) collective-permute-start(bf16[72,384]{1,0:T(8,128)(2,1)S(1)} %get-tuple-element.28), channel_id=1, source_target_pairs={{0,2},{2,4},{4,6},{6,0},{1,3},{3,5},{5,7},{7,1},{8,10},{10,12},{12... | collective-permute-start | bytes 165896 | tf_op jit(solution)/shard_map/ppermute | solution.py:263
  61.8 1.2 %collective-permute-start.4 = (f32[1,128]{1,0:T(1,128)S(1)}, f32[1,128]{1,0:T(1,128)S(1)}, u32[]{:S(2)}, u32[]{:S(2)}) collective-permute-start(f32[1,128]{1,0:T(1,128)S(1)} %get-tuple-element.23), channel_id=1, source_target_pairs={{0,1},{1,0},{2,3},{3,2},{4,5},{5,4},{6,7},{7,6},{8,9},{9,8},{10,11... | collective-permute-start | bytes 1544 | tf_op jit(solution)/shard_map/ppermute | solution.py:263

commit v4 on v3

--- a/solution.py
+++ b/solution.py
@@ -197,13 +197,10 @@
     return total[0], *[total[k].astype(BF) for k in range(1, own.shape[0])]
 
 
-def sigma_kernel(total_pairs, per, gathered, trial, gaps, kept, one, two, three, sigma, subspace, residuals, norms, grams):
+def sigma_kernel(total_pairs, stats, trial, gaps, kept, one, two, three, coupled_sum, rates, products, norms, grams):
     ys = 4
     y = lax.axis_index("y")
     vecs, rows = trial.shape
-    block = kept[:vecs, :]
-    for part in (one, two, three):
-        block = block + part[:vecs, :].astype(F32)
     for k, part in enumerate((kept, one, two, three)):
         grams[lax.rem(y + ys - k, ys)] = part[vecs:, :].astype(BF).astype(F32)
     strip = grams[0] + grams[1] + grams[2] + grams[3]
@@ -213,36 +210,33 @@
     turned = jnp.transpose(jnp.concatenate([corner, jnp.zeros((half, 128 - lanes), F32)], axis=1))
     lower = jnp.concatenate([turned[half:vecs], corner[:, vecs:]], axis=1)
     gram = jnp.concatenate([corner[:, :vecs], lower], axis=0)
-    groups, tall, _ = gathered.shape
-    base = tall - 8
-    wide = jnp.concatenate(
-        [gathered[j, base : base + per, :].astype(F32) + gathered[j, base + per : base + 2 * per, :].astype(F32) for j in range(groups)],
-        axis=0,
-    )
-    products = (wide[:, :vecs] + 2.0 * gram) / total_pairs
-    subspace[...] = products
+    wide = stats[...]
+    product = wide[:, :vecs] + 2.0 * gram
+    products[...] = product
     r = lax.broadcasted_iota(jnp.int32, (vecs, vecs), 0)
     q = lax.broadcasted_iota(jnp.int32, (vecs, vecs), 1)
-    diagonal = jnp.sum(jnp.where(r == q, products, 0.0), axis=1, keepdims=True)
-    rayleigh = diagonal / (wide[:, vecs : vecs + 1] / total_pairs + epsilon)
+    diagonal = jnp.sum(jnp.where(r == q, product, 0.0), axis=1, keepdims=True)
+    rayleigh = diagonal / total_pairs / (wide[:, vecs : vecs + 1] / total_pairs + epsilon)
+    rates[...] = jnp.broadcast_to(rayleigh, rates.shape)
+    block = kept[:vecs, :]
+    for part in (one, two, three):
+        block = block + part[:vecs, :].astype(F32)
+    coupled_sum[...] = block
     x = trial[...]
-    s = gaps[...] * x + 2.0 * block
-    sigma[...] = s
-    rest = s - rayleigh * x
-    residuals[...] = rest
+    rest = gaps[...] * x + 2.0 * block - rayleigh * x
     sums = jnp.sum(rest * rest, axis=1, keepdims=True)
     line = jnp.sum(jnp.where(r == q, jnp.broadcast_to(sums, (vecs, vecs)), 0.0), axis=0, keepdims=True)
     norms[...] = jnp.concatenate([line, jnp.zeros_like(line)], axis=1)
 
 
-def sigma_rows(total_pairs, per, gathered, trial, gaps, parts):
+def sigma_rows(total_pairs, stats, trial, gaps, parts):
     vecs, rows = trial.shape
     return pl.pallas_call(
-        lambda *refs: sigma_kernel(total_pairs, per, *refs),
+        lambda *refs: sigma_kernel(total_pairs, *refs),
         out_shape=[
             jax.ShapeDtypeStruct((vecs, rows), F32),
+            jax.ShapeDtypeStruct((vecs, 128), F32),
             jax.ShapeDtypeStruct((vecs, vecs), F32),
-            jax.ShapeDtypeStruct((vecs, rows), F32),
             jax.ShapeDtypeStruct((1, 128), F32),
         ],
         in_specs=[VMEM] * 7,
@@ -251,7 +245,24 @@
         compiler_params=pltpu.CompilerParams(vmem_limit_bytes=16 << 20),
         cost_estimate=pl.CostEstimate(flops=20 * trial.size, bytes_accessed=16 * trial.size, transcendentals=0),
         name="sigma_rows",
-    )(gathered, trial, gaps, *parts)
+    )(stats, trial, gaps, *parts)
+
+
+def finish_kernel(total_pairs, arrived, products, subspace, norms):
+    subspace[...] = products[...] / total_pairs
+    sums = jnp.sum(arrived[...], axis=0, keepdims=True)
+    norms[...] = jnp.sqrt(sums / total_pairs + epsilon)[:, : norms.shape[1]]
+
+
+def finish(total_pairs, arrived, products):
+    return pl.pallas_call(
+        lambda *refs: finish_kernel(total_pairs, *refs),
+        out_shape=[jax.ShapeDtypeStruct(products.shape, F32), jax.ShapeDtypeStruct((1, products.shape[0]), F32)],
+        in_specs=[VMEM] * 2,
+        out_specs=[VMEM] * 2,
+        compiler_params=pltpu.CompilerParams(vmem_limit_bytes=16 << 20),
+        name="finish",
+    )(arrived, products)
 
 
 def exchange(value, axis):
@@ -285,12 +296,20 @@
     mine, *sent = deal(own, arrived)
     far = shifted(sent[1], "y", 2)
     came = [shifted(sent[0], "y", 1), far, shifted(sent[2], "y", 3)]
-    sigma, subspace, residuals, norms = sigma_rows(total_pairs, per, gathered, own_trial, own_gaps, [mine, *came])
+    base = gathered.shape[1] - 8
+    stats = gathered[:, base : base + per, :].astype(F32) + gathered[:, base + per : base + 2 * per, :].astype(F32)
+    stats = stats.reshape(vecs, 128)
+    coupled_sum, rates, products, norms = sigma_rows(total_pairs, stats, own_trial, own_gaps, [mine, *came])
+    coupled_sum, own_trial, own_gaps = lax.optimization_barrier((coupled_sum, own_trial, own_gaps))
+    sigma = own_gaps * own_trial + 2.0 * coupled_sum
+    residuals = sigma - rates[:, :1] * own_trial
     norms = norms + shifted(norms, "c", 1)
+    norms, sigma, residuals = lax.optimization_barrier((norms, sigma, residuals))
     everyone = ("z", "x", "y")
     copies = jnp.broadcast_to(norms, (lax.axis_size(everyone), 1, 128))
-    sums = jnp.sum(exchange(copies, everyone), axis=(0, 1))[:vecs]
-    residual_norms = jnp.sqrt(sums / total_pairs + epsilon)
+    arrived = exchange(copies, everyone).reshape(-1, 128)
+    subspace, residual_norms = finish(total_pairs, arrived, products)
+    residual_norms = residual_norms.reshape(vecs)
     return (sigma.T, subspace, residuals.T, residual_norms)
 
 

time: 83.2 us -> 82.9 us (level)
  transfers between devices with their start and end apart: 6 -> 6, of which waited for: 6 -> 6; matrix products, arithmetic and copies ran while one was open for 4% -> 5% of each run, Pallas kernels for 0% -> 0%
where the time goes in v4:
time: 82.9 us; the launch traced here: 82 us
  blocking collectives  34.5 us (42%)
  starting transfers between devices  16.5 us (20%)
  waiting for transfers between devices  14.2 us (17%)
  Pallas kernels  11.3 us (14%)
  local copies, waits for them, and re-layouts  3.79 us (5%)
  other arithmetic  0.98 us (1%)
    all_to_all x2, blocking collectives, exchange(): return lax.all_to_all(value, axis, 0, 0, tiled=True)  34.5 us
    all_to_all x1, starting transfers between devices, exchange(): return lax.all_to_all(value, axis, 0, 0, tiled=True)  11.6 us
    all_to_all x1, waiting for transfers between devices, exchange(): return lax.all_to_all(value, axis, 0, 0, tiled=True)  7.61 us
    ppermute x5, waiting for transfers between devices, shifted(): return lax.ppermute(value, axis, [(i, (i + by) % n) for i in range(n)])  6.54 us
    pallas_call x1, Pallas kernels, totals(): pl.pallas_call(lambda *refs: totals_kernel(groups, *refs), out_shape=jax....  5.58 us
    ppermute x5, starting transfers between devices, shifted(): return lax.ppermute(value, axis, [(i, (i + by) % n) for i in range(n)])  4.88 us
    pallas_call x1, Pallas kernels, coupled(): pl.pallas_call(coupled_kernel, out_shape=[jax.ShapeDtypeStruct(shape, BF)...  4.62 us
    slice x1, local copies, waits for them, and re-layouts, local(): kept = lax.slice_in_dim(integrals, 0, pairs // ys, axis=0)  1.82 us
  transfers between devices with their start and end apart: 6, of which 6 were waited for; matrix products, arithmetic and copies ran while one was open for 5% of the time, Pallas kernels for 0%

profile of v4, /device:TPU:2, one launch (start us, length us, event | category | flops | bytes accessed | tf_op | source)
XLA Modules:
  0.0 82.0 jit_solution(5299825952052241811)
XLA Ops:
  0.6 5.6 %totals.1 = bf16[32,32,128]{2,1,0:T(8,128)(2,1)} custom-call(bf16[3072,1536]{1,0:T(8,128)(2,1)} %integrals.1, f32[64,3072]{1,0:T(8,128)} %bitcast.20, f32[1,3072]{1,0:T(1,128)} %bitcast.23), custom_call_target="tpu_custom_call" | custom-call | flops 2415919104 | bytes 9437184 | tf_op jit(solution)/shard_map/totals/pallas_call | solution.py:86
  6.2 11.6 %all-to-all-start = ((bf16[32,32,128]{2,1,0:T(8,128)(2,1)}), bf16[32,32,128]{2,1,0:T(8,128)(2,1)S(1)}, u32[]{:S(2)}, u32[]{:S(2)}) async-start(bf16[32,32,128]{2,1,0:T(8,128)(2,1)} %totals.1), calls=%async_computation | async-start | bytes 524288 | tf_op jit(solution)/shard_map/all_to_all | solution.py:269
  17.8 1.8 %slice.40.kept = bf16[768,1536]{1,0:T(8,128)(2,1)S(1)} slice(bf16[3072,1536]{1,0:T(8,128)(2,1)} %integrals.1), slice={[0:768], [0:1536]} | slice | bytes 4718592 | tf_op jit(solution)/shard_map/slice | solution.py:291
  19.7 0.8 dynamic-slice.7
  20.5 0.1 pad.3.clone
  20.5 0.9 %dynamic-slice_bitcast_fusion.refs_1_ = f32[64,384]{1,0:T(8,128)S(1)} fusion(f32[3072,64]{0,1:T(8,128)} %param.5, s32[]{:T(128)S(6)} %select_n.4), kind=kLoop, calls=%fused_computation.5 | loop fusion | bytes 196612 | tf_op jit(solution)/shard_map/dynamic_slice | solution.py:289
  21.4 7.6 %all-to-all-done = bf16[32,32,128]{2,1,0:T(8,128)(2,1)S(1)} async-done(((bf16[32,32,128]{2,1,0:T(8,128)(2,1)}), bf16[32,32,128]{2,1,0:T(8,128)(2,1)S(1)}, u32[]{:S(2)}, u32[]{:S(2)}) %all-to-all-start) | async-done | bytes 262176 | tf_op jit(solution)/shard_map/all_to_all | solution.py:269
  29.1 0.1 maximum_maximum_fusion
  29.3 15.8 %all_to_all.15.gathered = bf16[32,32,128]{2,1,0:T(8,128)(2,1)S(1)} all-to-all(bf16[32,32,128]{2,1,0:T(8,128)(2,1)S(1)} %broadcast_in_dim.13), channel_id=1, replica_groups=mesh['z'=8,'x'=4,'y'=4,'c'=2] {'z','x'}, dimensions={0} | all-to-all | bytes 524288 | tf_op jit(solution)/shard_map/all_to_all | solution.py:269
  45.1 4.6 %coupled.1 = (bf16[4,72,384]{2,1,0:T(8,128)(2,1)S(1)}, f32[4,72,384]{2,1,0:T(8,128)S(1)}) custom-call(bf16[3072,1536]{1,0:T(8,128)(2,1)} %integrals.1, bf16[768,1536]{1,0:T(8,128)(2,1)S(1)} %slice.40.kept, bf16[32,32,128]{2,1,0:T(8,128)(2,1)S(1)} %all_to_all.15.gathered), custom_call_target="tpu_custom_call" | custom-call | flops 2415919104 | bytes 9437184 | tf_op jit(solution)/shard_map/coupled/pallas_call | solution.py:176
  49.7 0.1 collective-permute-start
  49.8 1.4 %collective-permute-done = bf16[4,72,384]{2,1,0:T(8,128)(2,1)S(1)} collective-permute-done((bf16[4,72,384]{2,1,0:T(8,128)(2,1)S(1)}, bf16[4,72,384]{2,1,0:T(8,128)(2,1)S(1)}, u32[]{:S(2)}, u32[]{:S(2)}) %collective-permute-start) | collective-permute-done | bytes 221216 | tf_op jit(solution)/shard_map/ppermute | solution.py:274
  51.3 0.1 fusion.1
  51.4 3.1 %collective-permute-start.3 = (bf16[72,384]{1,0:T(8,128)(2,1)S(1)}, bf16[72,384]{1,0:T(8,128)(2,1)S(1)}, u32[]{:S(2)}, u32[]{:S(2)}) collective-permute-start(bf16[72,384]{1,0:T(8,128)(2,1)S(1)} %get-tuple-element.44), channel_id=1, source_target_pairs={{0,6},{2,0},{4,2},{6,4},{1,7},{3,1},{5,3},{7,5},{8,14},{10,8},{12,... | collective-permute-start | bytes 165896 | tf_op jit(solution)/shard_map/ppermute | solution.py:274
  54.5 0.6 collective-permute-start.2
  55.1 1.0 %collective-permute-start.1 = (bf16[72,384]{1,0:T(8,128)(2,1)S(1)}, bf16[72,384]{1,0:T(8,128)(2,1)S(1)}, u32[]{:S(2)}, u32[]{:S(2)}) collective-permute-start(bf16[72,384]{1,0:T(8,128)(2,1)S(1)} %get-tuple-element.46), channel_id=1, source_target_pairs={{0,2},{2,4},{4,6},{6,0},{1,3},{3,5},{5,7},{7,1},{8,10},{10,12},{12... | collective-permute-start | bytes 165896 | tf_op jit(solution)/shard_map/ppermute | solution.py:274
  56.1 0.6 collective-permute-done.3.refs_6_
  56.7 3.5 %collective-permute-done.2.refs_5_ = bf16[72,384]{1,0:T(8,128)(2,1)S(1)} collective-permute-done((bf16[72,384]{1,0:T(8,128)(2,1)S(1)}, bf16[72,384]{1,0:T(8,128)(2,1)S(1)}, u32[]{:S(2)}, u32[]{:S(2)}) %collective-permute-start.2) | collective-permute-done | bytes 55328 | tf_op jit(solution)/shard_map/ppermute | solution.py:274
  60.2 0.6 collective-permute-done.1.refs_4_
  60.8 0.4 sigma_rows.1
  61.2 0.1 slice_reduce_fusion
  61.3 0.1 collective-permute-start.4
  61.4 0.7 multiply_subtract_fusion
  62.2 0.4 collective-permute-done.4
  62.6 18.7 %all_to_all.16 = f32[128,1,128]{2,1,0:T(1,128)S(1)} all-to-all(f32[128,1,128]{2,1,0:T(1,128)S(1)} %broadcast_in_dim.14), channel_id=1, replica_groups=mesh['z'=8,'x'=4,'y'=4,'c'=2] {'z','x','y'}, dimensions={0} | all-to-all | bytes 131072 | tf_op jit(solution)/shard_map/all_to_all | solution.py:269
  81.3 0.6 finish.1
  (12 shorter events, 0.2 us)
Async XLA Ops:
  6.2 22.8 %all-to-all-start = ((bf16[32,32,128]{2,1,0:T(8,128)(2,1)}), bf16[32,32,128]{2,1,0:T(8,128)(2,1)S(1)}, u32[]{:S(2)}, u32[]{:S(2)}) async-start(bf16[32,32,128]{2,1,0:T(8,128)(2,1)} %totals.1), calls=%async_computation | async-start | bytes 524288 | tf_op jit(solution)/shard_map/all_to_all | solution.py:269
  49.7 1.6 %collective-permute-start = (bf16[4,72,384]{2,1,0:T(8,128)(2,1)S(1)}, bf16[4,72,384]{2,1,0:T(8,128)(2,1)S(1)}, u32[]{:S(2)}, u32[]{:S(2)}) collective-permute-start(bf16[4,72,384]{2,1,0:T(8,128)(2,1)S(1)} %get-tuple-element.27), channel_id=1, source_target_pairs={{0,1},{1,0},{2,3},{3,2},{4,5},{5,4},{6,7},{7,6},{8,9},{9,8},{10,11... | collective-permute-start | bytes 663560 | tf_op jit(solution)/shard_map/ppermute | solution.py:274
  51.4 5.3 %collective-permute-start.3 = (bf16[72,384]{1,0:T(8,128)(2,1)S(1)}, bf16[72,384]{1,0:T(8,128)(2,1)S(1)}, u32[]{:S(2)}, u32[]{:S(2)}) collective-permute-start(bf16[72,384]{1,0:T(8,128)(2,1)S(1)} %get-tuple-element.44), channel_id=1, source_target_pairs={{0,6},{2,0},{4,2},{6,4},{1,7},{3,1},{5,3},{7,5},{8,14},{10,8},{12,... | collective-permute-start | bytes 165896 | tf_op jit(solution)/shard_map/ppermute | solution.py:274
  54.5 5.7 %collective-permute-start.2 = (bf16[72,384]{1,0:T(8,128)(2,1)S(1)}, bf16[72,384]{1,0:T(8,128)(2,1)S(1)}, u32[]{:S(2)}, u32[]{:S(2)}) collective-permute-start(bf16[72,384]{1,0:T(8,128)(2,1)S(1)} %get-tuple-element.45), channel_id=1, source_target_pairs={{0,4},{2,6},{4,0},{6,2},{1,5},{3,7},{5,1},{7,3},{8,12},{10,14},{12... | collective-permute-start | bytes 165896 | tf_op jit(solution)/shard_map/ppermute | solution.py:274
  55.1 5.7 %collective-permute-start.1 = (bf16[72,384]{1,0:T(8,128)(2,1)S(1)}, bf16[72,384]{1,0:T(8,128)(2,1)S(1)}, u32[]{:S(2)}, u32[]{:S(2)}) collective-permute-start(bf16[72,384]{1,0:T(8,128)(2,1)S(1)} %get-tuple-element.46), channel_id=1, source_target_pairs={{0,2},{2,4},{4,6},{6,0},{1,3},{3,5},{5,7},{7,1},{8,10},{10,12},{12... | collective-permute-start | bytes 165896 | tf_op jit(solution)/shard_map/ppermute | solution.py:274
  61.3 1.2 %collective-permute-start.4 = (f32[1,128]{1,0:T(1,128)S(1)}, f32[1,128]{1,0:T(1,128)S(1)}, u32[]{:S(2)}, u32[]{:S(2)}) collective-permute-start(f32[1,128]{1,0:T(1,128)S(1)} %get-tuple-element.28), channel_id=1, source_target_pairs={{0,1},{1,0},{2,3},{3,2},{4,5},{5,4},{6,7},{7,6},{8,9},{9,8},{10,11... | collective-permute-start | bytes 1544 | tf_op jit(solution)/shard_map/ppermute | solution.py:274

commit v5 on v4

--- a/solution.py
+++ b/solution.py
@@ -235,7 +235,7 @@
         lambda *refs: sigma_kernel(total_pairs, *refs),
         out_shape=[
             jax.ShapeDtypeStruct((vecs, rows), F32),
-            jax.ShapeDtypeStruct((vecs, 128), F32),
+            jax.ShapeDtypeStruct((vecs, rows), F32),
             jax.ShapeDtypeStruct((vecs, vecs), F32),
             jax.ShapeDtypeStruct((1, 128), F32),
         ],
@@ -302,10 +302,10 @@
     coupled_sum, rates, products, norms = sigma_rows(total_pairs, stats, own_trial, own_gaps, [mine, *came])
     coupled_sum, own_trial, own_gaps = lax.optimization_barrier((coupled_sum, own_trial, own_gaps))
     sigma = own_gaps * own_trial + 2.0 * coupled_sum
-    residuals = sigma - rates[:, :1] * own_trial
+    residuals = sigma - rates * own_trial
     norms = norms + shifted(norms, "c", 1)
     norms, sigma, residuals = lax.optimization_barrier((norms, sigma, residuals))
-    everyone = ("z", "x", "y")
+    everyone = ("z", "y", "x")
     copies = jnp.broadcast_to(norms, (lax.axis_size(everyone), 1, 128))
     arrived = exchange(copies, everyone).reshape(-1, 128)
     subspace, residual_norms = finish(total_pairs, arrived, products)

time: 82.9 us -> 82.8 us (level)
  no operation moved by 1% of the time
where the time goes in v5:
time: 82.8 us; the launch traced here: 81.8 us
  blocking collectives  34.5 us (42%)
  starting transfers between devices  16.5 us (20%)
  waiting for transfers between devices  14.2 us (17%)
  Pallas kernels  11.3 us (14%)
  local copies, waits for them, and re-layouts  3.69 us (4%)
  other arithmetic  0.95 us (1%)
    all_to_all x2, blocking collectives, exchange(): return lax.all_to_all(value, axis, 0, 0, tiled=True)  34.5 us
    all_to_all x1, starting transfers between devices, exchange(): return lax.all_to_all(value, axis, 0, 0, tiled=True)  11.6 us
    all_to_all x1, waiting for transfers between devices, exchange(): return lax.all_to_all(value, axis, 0, 0, tiled=True)  7.61 us
    ppermute x5, waiting for transfers between devices, shifted(): return lax.ppermute(value, axis, [(i, (i + by) % n) for i in range(n)])  6.57 us
    pallas_call x1, Pallas kernels, totals(): pl.pallas_call(lambda *refs: totals_kernel(groups, *refs), out_shape=jax....  5.57 us
    ppermute x5, starting transfers between devices, shifted(): return lax.ppermute(value, axis, [(i, (i + by) % n) for i in range(n)])  4.87 us
    pallas_call x1, Pallas kernels, coupled(): pl.pallas_call(coupled_kernel, out_shape=[jax.ShapeDtypeStruct(shape, BF)...  4.63 us
    slice x1, local copies, waits for them, and re-layouts, local(): kept = lax.slice_in_dim(integrals, 0, pairs // ys, axis=0)  1.82 us
  transfers between devices with their start and end apart: 6, of which 6 were waited for; matrix products, arithmetic and copies ran while one was open for 5% of the time, Pallas kernels for 0%

profile of v5, /device:TPU:2, one launch (start us, length us, event | category | flops | bytes accessed | tf_op | source)
XLA Modules:
  0.0 81.8 jit_solution(7298058807691094245)
XLA Ops:
  0.6 5.6 %totals.1 = bf16[32,32,128]{2,1,0:T(8,128)(2,1)} custom-call(bf16[3072,1536]{1,0:T(8,128)(2,1)} %integrals.1, f32[64,3072]{1,0:T(8,128)} %bitcast.20, f32[1,3072]{1,0:T(1,128)} %bitcast.23), custom_call_target="tpu_custom_call" | custom-call | flops 2415919104 | bytes 9437184 | tf_op jit(solution)/shard_map/totals/pallas_call | solution.py:86
  6.2 11.6 %all-to-all-start = ((bf16[32,32,128]{2,1,0:T(8,128)(2,1)}), bf16[32,32,128]{2,1,0:T(8,128)(2,1)S(1)}, u32[]{:S(2)}, u32[]{:S(2)}) async-start(bf16[32,32,128]{2,1,0:T(8,128)(2,1)} %totals.1), calls=%async_computation | async-start | bytes 524288 | tf_op jit(solution)/shard_map/all_to_all | solution.py:269
  17.8 1.8 %slice.37.kept = bf16[768,1536]{1,0:T(8,128)(2,1)S(1)} slice(bf16[3072,1536]{1,0:T(8,128)(2,1)} %integrals.1), slice={[0:768], [0:1536]} | slice | bytes 4718592 | tf_op jit(solution)/shard_map/slice | solution.py:291
  19.7 0.8 dynamic-slice.7
  20.5 0.1 pad.3.clone
  20.5 0.9 %dynamic-slice_bitcast_fusion.refs_1_ = f32[64,384]{1,0:T(8,128)S(1)} fusion(f32[3072,64]{0,1:T(8,128)} %param.5, s32[]{:T(128)S(6)} %select_n.4), kind=kLoop, calls=%fused_computation.5 | loop fusion | bytes 196612 | tf_op jit(solution)/shard_map/dynamic_slice | solution.py:289
  21.4 7.6 %all-to-all-done = bf16[32,32,128]{2,1,0:T(8,128)(2,1)S(1)} async-done(((bf16[32,32,128]{2,1,0:T(8,128)(2,1)}), bf16[32,32,128]{2,1,0:T(8,128)(2,1)S(1)}, u32[]{:S(2)}, u32[]{:S(2)}) %all-to-all-start) | async-done | bytes 262176 | tf_op jit(solution)/shard_map/all_to_all | solution.py:269
  29.1 0.1 maximum_maximum_fusion
  29.2 15.8 %all_to_all.15.gathered = bf16[32,32,128]{2,1,0:T(8,128)(2,1)S(1)} all-to-all(bf16[32,32,128]{2,1,0:T(8,128)(2,1)S(1)} %broadcast_in_dim.13), channel_id=1, replica_groups=mesh['z'=8,'x'=4,'y'=4,'c'=2] {'z','x'}, dimensions={0} | all-to-all | bytes 524288 | tf_op jit(solution)/shard_map/all_to_all | solution.py:269
  45.1 4.6 %coupled.1 = (bf16[4,72,384]{2,1,0:T(8,128)(2,1)S(1)}, f32[4,72,384]{2,1,0:T(8,128)S(1)}) custom-call(bf16[3072,1536]{1,0:T(8,128)(2,1)} %integrals.1, bf16[768,1536]{1,0:T(8,128)(2,1)S(1)} %slice.37.kept, bf16[32,32,128]{2,1,0:T(8,128)(2,1)S(1)} %all_to_all.15.gathered), custom_call_target="tpu_custom_call" | custom-call | flops 2415919104 | bytes 9437184 | tf_op jit(solution)/shard_map/coupled/pallas_call | solution.py:176
  49.7 0.1 collective-permute-start
  49.8 1.4 %collective-permute-done = bf16[4,72,384]{2,1,0:T(8,128)(2,1)S(1)} collective-permute-done((bf16[4,72,384]{2,1,0:T(8,128)(2,1)S(1)}, bf16[4,72,384]{2,1,0:T(8,128)(2,1)S(1)}, u32[]{:S(2)}, u32[]{:S(2)}) %collective-permute-start) | collective-permute-done | bytes 221216 | tf_op jit(solution)/shard_map/ppermute | solution.py:274
  51.3 0.1 fusion.1
  51.4 3.1 %collective-permute-start.3 = (bf16[72,384]{1,0:T(8,128)(2,1)S(1)}, bf16[72,384]{1,0:T(8,128)(2,1)S(1)}, u32[]{:S(2)}, u32[]{:S(2)}) collective-permute-start(bf16[72,384]{1,0:T(8,128)(2,1)S(1)} %get-tuple-element.44), channel_id=1, source_target_pairs={{0,6},{2,0},{4,2},{6,4},{1,7},{3,1},{5,3},{7,5},{8,14},{10,8},{12,... | collective-permute-start | bytes 165896 | tf_op jit(solution)/shard_map/ppermute | solution.py:274
  54.4 0.6 collective-permute-start.2
  55.1 1.0 %collective-permute-start.1 = (bf16[72,384]{1,0:T(8,128)(2,1)S(1)}, bf16[72,384]{1,0:T(8,128)(2,1)S(1)}, u32[]{:S(2)}, u32[]{:S(2)}) collective-permute-start(bf16[72,384]{1,0:T(8,128)(2,1)S(1)} %get-tuple-element.46), channel_id=1, source_target_pairs={{0,2},{2,4},{4,6},{6,0},{1,3},{3,5},{5,7},{7,1},{8,10},{10,12},{12... | collective-permute-start | bytes 165896 | tf_op jit(solution)/shard_map/ppermute | solution.py:274
  56.1 0.6 collective-permute-done.3.refs_6_
  56.7 3.5 %collective-permute-done.2.refs_5_ = bf16[72,384]{1,0:T(8,128)(2,1)S(1)} collective-permute-done((bf16[72,384]{1,0:T(8,128)(2,1)S(1)}, bf16[72,384]{1,0:T(8,128)(2,1)S(1)}, u32[]{:S(2)}, u32[]{:S(2)}) %collective-permute-start.2) | collective-permute-done | bytes 55328 | tf_op jit(solution)/shard_map/ppermute | solution.py:274
  60.2 0.6 collective-permute-done.1.refs_4_
  60.8 0.4 sigma_rows.1
  61.2 0.1 collective-permute-start.4
  61.3 0.7 multiply_subtract_fusion
  62.0 0.4 collective-permute-done.4
  62.5 18.7 %all_to_all.16 = f32[128,1,128]{2,1,0:T(1,128)S(1)} all-to-all(f32[128,1,128]{2,1,0:T(1,128)S(1)} %broadcast_in_dim.14), channel_id=1, replica_groups=mesh['z'=8,'x'=4,'y'=4,'c'=2] {'z','y','x'}, dimensions={0} | all-to-all | bytes 131072 | tf_op jit(solution)/shard_map/all_to_all | solution.py:269
  81.2 0.6 finish.1
  (12 shorter events, 0.2 us)
Async XLA Ops:
  6.2 22.8 %all-to-all-start = ((bf16[32,32,128]{2,1,0:T(8,128)(2,1)}), bf16[32,32,128]{2,1,0:T(8,128)(2,1)S(1)}, u32[]{:S(2)}, u32[]{:S(2)}) async-start(bf16[32,32,128]{2,1,0:T(8,128)(2,1)} %totals.1), calls=%async_computation | async-start | bytes 524288 | tf_op jit(solution)/shard_map/all_to_all | solution.py:269
  49.7 1.6 %collective-permute-start = (bf16[4,72,384]{2,1,0:T(8,128)(2,1)S(1)}, bf16[4,72,384]{2,1,0:T(8,128)(2,1)S(1)}, u32[]{:S(2)}, u32[]{:S(2)}) collective-permute-start(bf16[4,72,384]{2,1,0:T(8,128)(2,1)S(1)} %get-tuple-element.27), channel_id=1, source_target_pairs={{0,1},{1,0},{2,3},{3,2},{4,5},{5,4},{6,7},{7,6},{8,9},{9,8},{10,11... | collective-permute-start | bytes 663560 | tf_op jit(solution)/shard_map/ppermute | solution.py:274
  51.4 5.3 %collective-permute-start.3 = (bf16[72,384]{1,0:T(8,128)(2,1)S(1)}, bf16[72,384]{1,0:T(8,128)(2,1)S(1)}, u32[]{:S(2)}, u32[]{:S(2)}) collective-permute-start(bf16[72,384]{1,0:T(8,128)(2,1)S(1)} %get-tuple-element.44), channel_id=1, source_target_pairs={{0,6},{2,0},{4,2},{6,4},{1,7},{3,1},{5,3},{7,5},{8,14},{10,8},{12,... | collective-permute-start | bytes 165896 | tf_op jit(solution)/shard_map/ppermute | solution.py:274
  54.4 5.7 %collective-permute-start.2 = (bf16[72,384]{1,0:T(8,128)(2,1)S(1)}, bf16[72,384]{1,0:T(8,128)(2,1)S(1)}, u32[]{:S(2)}, u32[]{:S(2)}) collective-permute-start(bf16[72,384]{1,0:T(8,128)(2,1)S(1)} %get-tuple-element.45), channel_id=1, source_target_pairs={{0,4},{2,6},{4,0},{6,2},{1,5},{3,7},{5,1},{7,3},{8,12},{10,14},{12... | collective-permute-start | bytes 165896 | tf_op jit(solution)/shard_map/ppermute | solution.py:274
  55.1 5.7 %collective-permute-start.1 = (bf16[72,384]{1,0:T(8,128)(2,1)S(1)}, bf16[72,384]{1,0:T(8,128)(2,1)S(1)}, u32[]{:S(2)}, u32[]{:S(2)}) collective-permute-start(bf16[72,384]{1,0:T(8,128)(2,1)S(1)} %get-tuple-element.46), channel_id=1, source_target_pairs={{0,2},{2,4},{4,6},{6,0},{1,3},{3,5},{5,7},{7,1},{8,10},{10,12},{12... | collective-permute-start | bytes 165896 | tf_op jit(solution)/shard_map/ppermute | solution.py:274
  61.2 1.2 %collective-permute-start.4 = (f32[1,128]{1,0:T(1,128)S(1)}, f32[1,128]{1,0:T(1,128)S(1)}, u32[]{:S(2)}, u32[]{:S(2)}) collective-permute-start(f32[1,128]{1,0:T(1,128)S(1)} %get-tuple-element.28), channel_id=1, source_target_pairs={{0,1},{1,0},{2,3},{3,2},{4,5},{5,4},{6,7},{7,6},{8,9},{9,8},{10,11... | collective-permute-start | bytes 1544 | tf_op jit(solution)/shard_map/ppermute | solution.py:274
